TPU v7x, 256 devices: a whole 4x4x8 slice. The times are simulated.
256 devices in a mesh: dp: 4 (over x), expert: 64 (over y, z, core).
Axes of the slice: x: 4, y: 4, z: 8, core: 2. Of those that a mesh axis runs over, the one named last changes fastest.
Arguments:
- tokens: bfloat16 [32768, 2048], P(('dp', 'expert')), may hold values from -24 to 24
- grad_out: bfloat16 [32768, 2048], P(('dp', 'expert')), may hold values from -0.125 to 0.125
- router_weight: bfloat16 [2048, 64], replicated, may hold values from -0.125 to 0.125
- expert_index: int32 [32768, 8], P(('dp', 'expert')), may hold values from 0 to 63, all different within a row; in each aligned block of 128 rows (0 to 127, 128 to 255, ...) at most 24 rows name the same one
- w_gate: bfloat16 [64, 2048, 768], P('expert'), may hold values from -0.125 to 0.125
- w_up: bfloat16 [64, 2048, 768], P('expert'), may hold values from -0.125 to 0.125
- w_down: bfloat16 [64, 768, 2048], P('expert'), may hold values from -0.21875 to 0.21875
Outputs:
- gate_grad: float32 [32768, 8], P(('dp', 'expert'))
- router_grad: float32 [2048, 64], P('expert')
Inputs may be any that keep to these rules, and one draw needn't show every extreme that they name: `expert_index`: each row names 8 different experts. In each aligned block of 128 rows (the rows of one device) no expert is named by more than 24 rows, a bound that some blocks reach.
All inputs are finite; a program needn't handle non-finite values.
Results may differ from a plain program's by a relative error of at most 0.009.
Values may be sent and summed in bfloat16 or wider, within the bound.
No kernel may reach another device: no remote copies, remote signals or barrier semaphores. Data moves between devices by JAX's collectives and lax.ppermute only.
A program may use at most 128 MiB of HBM per device.

v0:
```python
import functools

import jax
import jax.numpy as jnp
import numpy as np
from jax import lax
from jax.experimental import pallas as pl
from jax.experimental.pallas import tpu as pltpu
from jax.sharding import Mesh, PartitionSpec as P


NY, NZ, NC = 4, 8, 2
CAP = 24
PACK, STRIDE = 4, 32
VMEM = 48 * 1024 * 1024


def params():
    return pltpu.CompilerParams(vmem_limit_bytes=VMEM)


def in_vmem(count):
    return [pl.BlockSpec(memory_space=pltpu.VMEM)] * count


def in_smem():
    return [pl.BlockSpec(memory_space=pltpu.SMEM)]


def pack_kernel(tok_ref, grad_ref, idx_ref, out_ref):
    rows, width = tok_ref.shape
    out_ref[:, :width] = tok_ref[...]
    out_ref[:, width : 2 * width] = grad_ref[...]
    lane = lax.broadcasted_iota(jnp.int32, (rows, 128), 1)
    hit = jnp.zeros((rows, 128), jnp.float32)
    for k in range(idx_ref.shape[1]):
        hit = hit + (idx_ref[:, k : k + 1] == lane).astype(jnp.float32)
    earlier = lax.broadcasted_iota(jnp.int32, (rows, rows), 0) > lax.broadcasted_iota(
        jnp.int32, (rows, rows), 1
    )
    before = jnp.dot(
        earlier.astype(jnp.bfloat16),
        hit.astype(jnp.bfloat16),
        preferred_element_type=jnp.float32,
    )
    out_ref[:, 2 * width :] = jnp.where(hit > 0.0, before, -1.0).astype(jnp.bfloat16)


def pick_kernel(count, here_ref, *refs):
    slices, outs, chosen_ref = refs[:count], refs[count:-1], refs[-1]
    y, z, c = here_ref[0], here_ref[1], here_ref[2]
    width = outs[0].shape[1]
    slots = NY * CAP
    column = lax.broadcasted_iota(jnp.int32, (128, slots), 1)
    row = lax.broadcasted_iota(jnp.int32, (128, slots), 0)
    expert = jnp.zeros((128, slots), jnp.int32)
    slot = column
    for dy in range(NY):
        number = ((y + dy) % NY) * (NZ * NC) + z * NC + c
        expert = jnp.where(column >= dy * CAP, number, expert)
        slot = jnp.where(column >= dy * CAP, column - dy * CAP, slot)
    choose = (row == expert).astype(jnp.bfloat16)
    slot = slot.astype(jnp.float32)
    for i in range(count):
        place = slices[i][:, width:]
        spread = jnp.dot(place, choose, preferred_element_type=jnp.float32)
        chosen_ref[i] = (spread == slot).astype(jnp.float32).T.astype(jnp.bfloat16)

    tile = 1024

    @pl.loop(0, width // tile)
    def _(step):
        cols = pl.ds(pl.multiple_of(step * tile, tile), tile)
        for i in range(count):
            taken = jnp.dot(
                chosen_ref[i], slices[i][:, cols], preferred_element_type=jnp.float32
            )
            for dy in range(NY):
                outs[dy][i * CAP : (i + 1) * CAP, cols] = taken[
                    dy * CAP : (dy + 1) * CAP
                ].astype(jnp.bfloat16)


def pick(here, slices):
    count = len(slices)
    rows, width = slices[0].shape[0], slices[0].shape[1] - 128
    return pl.pallas_call(
        functools.partial(pick_kernel, count),
        out_shape=[jax.ShapeDtypeStruct((count * CAP, width), jnp.bfloat16)] * NY,
        in_specs=in_smem() + in_vmem(count),
        out_specs=in_vmem(NY),
        scratch_shapes=[pltpu.VMEM((count, NY * CAP, rows), jnp.bfloat16)],
        compiler_params=params(),
        cost_estimate=pl.CostEstimate(
            flops=2 * 96 * 128 * 4096 * count, bytes_accessed=2 * count << 20, transcendentals=0
        ),
    )(here, *slices)


def expert_kernel(steps, chunk, table_ref, *refs):
    (*ins, gate_ref, up_ref, down_ref, before_ref, out_ref, toks, grads, total) = refs
    rows, width = toks.shape
    step = pl.program_id(0)

    @pl.when(step == 0)
    def _():
        at = 0
        for part in ins:
            toks[at : at + part.shape[0], :] = part[:, :width]
            grads[at : at + part.shape[0], :] = part[:, width:]
            at += part.shape[0]

    @pl.loop(0, rows // chunk)
    def _(i):
        own = pl.ds(pl.multiple_of(i * chunk, chunk), chunk)
        x = toks[own, :]
        gate_in = jnp.dot(x, gate_ref[...], preferred_element_type=jnp.float32)
        up_in = jnp.dot(x, up_ref[...], preferred_element_type=jnp.float32)
        hidden = (gate_in / (1.0 + jnp.exp(-gate_in)) * up_in).astype(jnp.bfloat16)
        term = jnp.dot(hidden, down_ref[...], preferred_element_type=jnp.float32)

        @pl.when(step == 0)
        def _():
            total[own, :] = term

        @pl.when(step > 0)
        def _():
            total[own, :] += term

    @pl.when(step == steps - 1)
    def _():
        out_ref[...] = before_ref[...]
        lane = lax.broadcasted_iota(jnp.int32, (CAP, 128), 1)
        row = lax.broadcasted_iota(jnp.int32, (CAP, 128), 0)

        @pl.loop(0, rows // (2 * CAP))
        def _(pair):
            first = pl.multiple_of(pair * (2 * CAP), 2 * CAP)
            made = total[pl.ds(first, 2 * CAP), :].astype(jnp.bfloat16).astype(jnp.float32)
            grad = grads[pl.ds(first, 2 * CAP), :].astype(jnp.float32)
            dots = jnp.sum(made * grad, axis=1, keepdims=True)
            for half in range(2):
                home = table_ref[0, 2 * pair + half]
                source = table_ref[1, 2 * pair + half]
                mine = dots[half * CAP : (half + 1) * CAP]
                at_lane = row + (source % PACK) * STRIDE
                line = jnp.sum(jnp.where(at_lane == lane, mine, 0.0), axis=0, keepdims=True)
                out_ref[home, pl.ds(source // PACK, 1), :] += line


def expert(table, parts, gate_w, up_w, down_w, before):
    width, inner = gate_w.shape
    tile = 256
    steps = inner // tile
    rows = sum(part.shape[0] for part in parts)
    chunk = rows if rows <= 384 else rows // 2
    return pl.pallas_call(
        functools.partial(expert_kernel, steps, chunk),
        grid=(steps,),
        out_shape=jax.ShapeDtypeStruct(before.shape, jnp.float32),
        in_specs=in_smem()
        + [pl.BlockSpec(part.shape, lambda f: (0, 0)) for part in parts]
        + [
            pl.BlockSpec((width, tile), lambda f: (0, f)),
            pl.BlockSpec((width, tile), lambda f: (0, f)),
            pl.BlockSpec((tile, width), lambda f: (f, 0)),
            pl.BlockSpec(before.shape, lambda f: (0, 0, 0)),
        ],
        out_specs=pl.BlockSpec(before.shape, lambda f: (0, 0, 0)),
        scratch_shapes=[
            pltpu.VMEM((rows, width), jnp.bfloat16),
            pltpu.VMEM((rows, width), jnp.bfloat16),
            pltpu.VMEM((rows, width), jnp.float32),
        ],
        compiler_params=params(),
        cost_estimate=pl.CostEstimate(
            flops=6 * rows * width * inner, bytes_accessed=12 << 20, transcendentals=rows * inner
        ),
    )(table, *parts, gate_w, up_w, down_w, before)


def side_kernel(here_ref, *refs):
    slices, router_ref, gates_ref, place_ref, feats_ref = refs[:NZ], *refs[NZ:]
    z = here_ref[1]
    rows = slices[0].shape[0]
    width, experts = router_ref.shape
    router = router_ref[...]
    for j in range(NZ):
        source = (z + j) % NZ
        place = slices[j][:, 2 * width :].astype(jnp.float32)[:, :experts]
        logits = jnp.dot(slices[j][:, :width], router, preferred_element_type=jnp.float32)
        hit = place >= 0.0
        weights = jnp.where(hit, jnp.exp(jnp.where(hit, logits, 0.0)), 0.0)
        gates_ref[source] = weights / jnp.sum(weights, axis=1, keepdims=True)
        place_ref[source] = place
        at = pl.multiple_of(source * rows, rows)
        for y in range(NY):
            col = pl.multiple_of(y * (width // NY) + (z // 2) * 128, 128)
            feats_ref[pl.ds(at, rows), y * 128 : (y + 1) * 128] = slices[j][:, pl.ds(col, 128)]


def side(here, slices, router_weight):
    rows, experts = slices[0].shape[0], router_weight.shape[1]
    return pl.pallas_call(
        side_kernel,
        out_shape=[
            jax.ShapeDtypeStruct((NZ, rows, experts), jnp.float32),
            jax.ShapeDtypeStruct((NZ, rows, experts), jnp.float32),
            jax.ShapeDtypeStruct((NZ * rows, NY * 128), jnp.bfloat16),
        ],
        in_specs=in_smem() + in_vmem(NZ + 1),
        out_specs=in_vmem(3),
        compiler_params=params(),
        cost_estimate=pl.CostEstimate(
            flops=2 * NZ * rows * 2048 * 256, bytes_accessed=6 << 20, transcendentals=NZ * rows * 64
        ),
    )(here, *slices, router_weight)


def finish_kernel(
    here_ref, back_ref, gates_ref, place_ref, feats_ref, idx_ref,
    grad_ref, part_ref, table_ref, wide_ref, dense_ref, sum_ref,
):
    z = here_ref[1]
    rows, experts = gates_ref.shape[1:]
    for a in range(NZ // PACK):
        table_ref[a * 128 : (a + 1) * 128, :] = back_ref[:, a, :].T

    @pl.loop(0, NZ)
    def _(source):
        place = place_ref[source]
        lines = table_ref[pl.ds(pl.multiple_of(source * STRIDE, STRIDE), STRIDE), :]
        wide = jnp.zeros((rows, experts), jnp.float32)
        for s in range(CAP):
            wide = jnp.where(place == float(s), lines[s : s + 1, :], wide)
        wide_ref[source] = wide
        gates = gates_ref[source]
        mean = jnp.sum(gates * wide, axis=1, keepdims=True)
        at = pl.multiple_of(source * rows, rows)
        dense_ref[pl.ds(at, rows), :] = (gates * (wide - mean)).astype(jnp.bfloat16)

    part = lax.dot_general(
        dense_ref[...],
        feats_ref[...],
        (((0,), (0,)), ((), ())),
        preferred_element_type=jnp.float32,
    )
    sum_ref[...] = part.T
    half = 16
    for y in range(NY):
        for c in range(NC):
            at = pl.multiple_of(y * 128 + (z % 2) * 64 + c * 32, 32)
            for copy in range(part_ref.shape[0]):
                part_ref[copy, y * NC + c, :, :experts] = sum_ref[pl.ds(at, half), :]
                part_ref[copy, y * NC + c, :, experts:] = sum_ref[pl.ds(at + half, half), :]
    own = wide_ref[z]
    number = lax.broadcasted_iota(jnp.int32, (rows, experts), 1)
    lane = lax.broadcasted_iota(jnp.int32, grad_ref.shape, 1)
    out = jnp.zeros(grad_ref.shape, jnp.float32)
    for k in range(grad_ref.shape[1]):
        here_k = idx_ref[:, k : k + 1] == number
        value = jnp.sum(jnp.where(here_k, own, 0.0), axis=1, keepdims=True)
        out = jnp.where(lane == k, value, out)
    grad_ref[...] = out


def finish(here, back, gates, place, feats, expert_index, copies):
    rows, top = expert_index.shape
    experts = gates.shape[2]
    return pl.pallas_call(
        finish_kernel,
        out_shape=[
            jax.ShapeDtypeStruct((rows, top), jnp.float32),
            jax.ShapeDtypeStruct((copies, NY * NC, 16, 2 * experts), jnp.float32),
        ],
        in_specs=in_smem() + in_vmem(5),
        out_specs=in_vmem(2),
        scratch_shapes=[
            pltpu.VMEM((NZ * STRIDE, experts), jnp.float32),
            pltpu.VMEM((NZ, rows, experts), jnp.float32),
            pltpu.VMEM((NZ * rows, experts), jnp.bfloat16),
            pltpu.VMEM((NY * 128, experts), jnp.float32),
        ],
        compiler_params=params(),
        cost_estimate=pl.CostEstimate(flops=1 << 28, bytes_accessed=3 << 20, transcendentals=0),
    )(here, back, gates, place, feats, expert_index)


def sum_kernel(parts_ref, out_ref):
    total = parts_ref[0]
    for i in range(1, parts_ref.shape[0]):
        total = total + parts_ref[i]
    half, lanes = total.shape
    out_ref[:half, :] = total[:, : lanes // 2]
    out_ref[half:, :] = total[:, lanes // 2 :]


def shifted(array, axis, by):
    size = lax.axis_size(axis)
    return lax.ppermute(array, axis, [(i, (i + by) % size) for i in range(size)])


def on_device(tokens, grad_out, router_weight, expert_index, w_gate, w_up, w_down):
    tok_rows, width = tokens.shape
    experts = router_weight.shape[1]
    y, z, c = (lax.axis_index(a) for a in ("y", "z", "c"))
    here = jnp.stack([y, z, c]).astype(jnp.int32)
    packed = pl.pallas_call(
        pack_kernel,
        out_shape=jax.ShapeDtypeStruct((tok_rows, 2 * width + 128), jnp.bfloat16),
        compiler_params=params(),
    )(tokens, grad_out, expert_index)

    last = NZ // 2
    ups, downs = {0: packed}, {0: packed}
    for step in range(1, last + 1):
        ups[step] = shifted(ups[step - 1], "z", 1)
        if step < last:
            downs[step] = shifted(downs[step - 1], "z", -1)
    stops, arrived = [], []
    for step in range(last + 1):
        if step == 0 or step == last:
            stops.append((step,))
            slices = [ups[step]]
        else:
            stops.append((NZ - step, step))
            slices = [ups[step], downs[step]]
        slices = slices + [shifted(a, "c", 1) for a in slices]
        rows = pick(here, slices)
        arrived.append([rows[0]] + [shifted(rows[dy], "y", dy) for dy in range(1, NY)])

    products = jnp.zeros((NY * NC, NZ // PACK, 128), jnp.float32)
    for steps in ((0, 1), (2,), (3,), (4,)):
        parts, table = [], []
        for step in steps:
            for dy in range(NY):
                parts.append(arrived[step][dy])
                for core in range(NC):
                    for offset in stops[step]:
                        table.append((dy, core, offset))
        dys, cores, offsets = np.array(table, np.int32).T
        homes = jnp.stack([(y + NY - dys) % NY * NC + (c + cores) % NC, (z + offsets) % NZ])
        products = expert(homes, parts, w_gate[0], w_up[0], w_down[0], products)
    columns = [ups[0]] + [downs[j] for j in range(1, last)] + [ups[last]]
    columns += [ups[j] for j in range(last - 1, 0, -1)]
    gates, place, feats = side(here, columns, router_weight)

    back = products.reshape(NY, 1, NC, NZ // PACK, 128)
    back = jnp.broadcast_to(back, (NY, NZ, NC, NZ // PACK, 128)).reshape(experts, NZ // PACK, 128)
    back = lax.all_to_all(back, ("y", "z", "c"), 0, 0, tiled=True)
    copies = lax.axis_size("dp")
    gate_grad, part = finish(here, back, gates, place, feats, expert_index, copies)
    parts = lax.all_to_all(
        part.reshape(copies * NY * NC, 16, 2 * experts), ("dp", "y", "c"), 0, 0, tiled=True
    )
    router_grad = pl.pallas_call(
        sum_kernel, out_shape=jax.ShapeDtypeStruct((32, experts), jnp.float32)
    )(parts)
    return (gate_grad, router_grad)


def solution(mesh):
    devices = mesh.devices.reshape(mesh.devices.shape[0], NY, NZ, NC)
    fine = Mesh(devices, ("dp", "y", "z", "c"))
    rows = P(("dp", "y", "z", "c"), None)
    own = P(("y", "z", "c"), None, None)

    return jax.shard_map(
        on_device,
        mesh=fine,
        in_specs=(rows, rows, P(), rows, own, own, own),
        out_specs=(rows, P(("y", "z", "c"), None)),
        check_vma=False,
    )
```

profile of v0, /device:TPU:1, one launch (start us, length us, event | category | flops | bytes accessed | tf_op | source)
XLA Modules:
  0.0 273.6 jit_solution(14379788086111906555)
XLA Ops:
  1.4 1.0 copy-done.12
  2.5 1.0 copy-done.13
  3.9 2.5 collective-permute-start
  6.4 4.0 %collective-permute-start.8 = (bf16[128,4224]{1,0:T(8,128)(2,1)S(1)}, bf16[128,4224]{1,0:T(8,128)(2,1)S(1)}, u32[]{:S(2)}, u32[]{:S(2)}) collective-permute-start(bf16[128,4224]{1,0:T(8,128)(2,1)S(1)} %shard_map.194.refs_0_), channel_id=1, source_target_pairs={{0,14},{2,0},{4,2},{6,4},{8,6},{10,8},{12,10},{14,12},{1,15},{3,1}... | collective-permute-start | bytes 3244040 | tf_op jit(solution)/shard_map/ppermute | solution.py:300
  11.3 22.5 %collective-permute-done.refs_0_.refs_7_ = bf16[128,4224]{1,0:T(8,128)(2,1)S(1)} collective-permute-done((bf16[128,4224]{1,0:T(8,128)(2,1)S(1)}, bf16[128,4224]{1,0:T(8,128)(2,1)S(1)}, u32[]{:S(2)}, u32[]{:S(2)}) %collective-permute-start) | collective-permute-done | bytes 1081376 | tf_op jit(solution)/shard_map/ppermute | solution.py:300
  33.9 2.7 collective-permute-start.9
  36.6 2.5 shard_map.198
  39.9 1.3 collective-permute-start.22
  41.2 2.1 collective-permute-start.25
  43.3 16.0 %collective-permute-done.1.refs_0_.refs_6_ = bf16[128,4224]{1,0:T(8,128)(2,1)} collective-permute-done((bf16[128,4224]{1,0:T(8,128)(2,1)S(1)}, bf16[128,4224]{1,0:T(8,128)(2,1)}, u32[]{:S(2)}, u32[]{:S(2)}) %collective-permute-start.1) | collective-permute-done | bytes 1081376 | tf_op jit(solution)/shard_map/ppermute | solution.py:300
  59.4 2.1 collective-permute-start.26
  62.2 2.9 %collective-permute-start.23 = (bf16[48,4096]{1,0:T(8,128)(2,1)S(1)}, bf16[48,4096]{1,0:T(8,128)(2,1)S(1)}, u32[]{:S(2)}, u32[]{:S(2)}) collective-permute-start(bf16[48,4096]{1,0:T(8,128)(2,1)S(1)} %get-tuple-element.41), channel_id=1, source_target_pairs={{0,32},{16,48},{32,0},{48,16},{1,33},{17,49},{33,1},{49,17},{2,34}... | collective-permute-start | bytes 1179656 | tf_op jit(solution)/shard_map/ppermute | solution.py:300
  65.1 3.0 %collective-permute-start.10 = (bf16[128,4224]{1,0:T(8,128)(2,1)}, bf16[128,4224]{1,0:T(8,128)(2,1)}, u32[]{:S(2)}, u32[]{:S(2)}) collective-permute-start(bf16[128,4224]{1,0:T(8,128)(2,1)} %collective-permute-done.9.refs_1_.refs_2_), channel_id=1, source_target_pairs={{0,14},{2,0},{4,2},{6,4},{8,6},{10,8},{12,10},{14,12},{1,15},{3,1}... | collective-permute-start | bytes 3244040 | tf_op jit(solution)/shard_map/ppermute | solution.py:300
  68.1 6.3 %collective-permute-done.23.refs_2_ = bf16[48,4096]{1,0:T(8,128)(2,1)S(1)} collective-permute-done((bf16[48,4096]{1,0:T(8,128)(2,1)S(1)}, bf16[48,4096]{1,0:T(8,128)(2,1)S(1)}, u32[]{:S(2)}, u32[]{:S(2)}) %collective-permute-start.23) | collective-permute-done | bytes 393248 | tf_op jit(solution)/shard_map/ppermute | solution.py:300
  75.1 2.7 collective-permute-start.24
  77.8 7.6 %collective-permute-done.24.refs_3_ = bf16[48,4096]{1,0:T(8,128)(2,1)S(1)} collective-permute-done((bf16[48,4096]{1,0:T(8,128)(2,1)S(1)}, bf16[48,4096]{1,0:T(8,128)(2,1)S(1)}, u32[]{:S(2)}, u32[]{:S(2)}) %collective-permute-start.24) | collective-permute-done | bytes 393248 | tf_op jit(solution)/shard_map/ppermute | solution.py:300
  86.2 1.7 collective-permute-start.16
  88.5 2.8 %collective-permute-done.10.refs_1_.refs_3_ = bf16[128,4224]{1,0:T(8,128)(2,1)} collective-permute-done((bf16[128,4224]{1,0:T(8,128)(2,1)}, bf16[128,4224]{1,0:T(8,128)(2,1)}, u32[]{:S(2)}, u32[]{:S(2)}) %collective-permute-start.10) | collective-permute-done | bytes 1081376 | tf_op jit(solution)/shard_map/ppermute | solution.py:300
  91.3 1.1 collective-permute-start.12
  92.5 1.2 copy-done.3
  93.7 4.7 %shard_map.199 = (bf16[96,4096]{1,0:T(8,128)(2,1)S(1)}, bf16[96,4096]{1,0:T(8,128)(2,1)}, bf16[96,4096]{1,0:T(8,128)(2,1)}, bf16[96,4096]{1,0:T(8,128)(2,1)}) custom-call(s32[3]{0:T(128)S(1)} %pad_add_fusion.3.here_ref, bf16[128,4224]{1,0:T(8,128)(2,1)S(1)} %collective-permute-done.refs_0_.refs_7_, bf16[128,4224]{1,0:T(8,128)(2,1)S(1)} %copy-done.3, ...), custom_call_target="tpu_custom_call" | custom-call | flops 402653184 | bytes 8388608 | tf_op jit(solution)/shard_map/pallas_call | solution.py:87
  99.7 1.6 collective-permute-start.28
  102.2 13.5 %collective-permute-done.3.refs_0_.refs_4_ = bf16[128,4224]{1,0:T(8,128)(2,1)S(1)} collective-permute-done((bf16[128,4224]{1,0:T(8,128)(2,1)S(1)}, bf16[128,4224]{1,0:T(8,128)(2,1)S(1)}, u32[]{:S(2)}, u32[]{:S(2)}) %collective-permute-start.3) | collective-permute-done | bytes 1081376 | tf_op jit(solution)/shard_map/ppermute | solution.py:300
  116.4 5.4 %shard_map.197 = (bf16[96,4096]{1,0:T(8,128)(2,1)S(1)}, bf16[96,4096]{1,0:T(8,128)(2,1)}, bf16[96,4096]{1,0:T(8,128)(2,1)}, bf16[96,4096]{1,0:T(8,128)(2,1)}) custom-call(s32[3]{0:T(128)S(1)} %pad_add_fusion.3.here_ref, bf16[128,4224]{1,0:T(8,128)(2,1)} %collective-permute-done.1.refs_0_.refs_6_, bf16[128,4224]{1,0:T(8,128)(2,1)} %collective-permute-done.9.refs_1_.refs_2_, ...), custom_call_target="tpu_custom_call" | custom-call | flops 402653184 | bytes 8388608 | tf_op jit(solution)/shard_map/pallas_call | solution.py:87
  123.7 4.5 %shard_map.196 = (bf16[96,4096]{1,0:T(8,128)(2,1)S(1)}, bf16[96,4096]{1,0:T(8,128)(2,1)}, bf16[96,4096]{1,0:T(8,128)(2,1)S(1)}, bf16[96,4096]{1,0:T(8,128)(2,1)S(1)}) custom-call(s32[3]{0:T(128)S(1)} %pad_add_fusion.3.here_ref, bf16[128,4224]{1,0:T(8,128)(2,1)S(1)} %copy-done.6, bf16[128,4224]{1,0:T(8,128)(2,1)} %collective-permute-done.10.refs_1_.refs_3_, ...), custom_call_target="tpu_custom_call" | custom-call | flops 402653184 | bytes 8388608 | tf_op jit(solution)/shard_map/pallas_call | solution.py:87
  130.9 5.6 %collective-permute-done.27.refs_5_ = bf16[96,4096]{1,0:T(8,128)(2,1)} collective-permute-done((bf16[96,4096]{1,0:T(8,128)(2,1)}, bf16[96,4096]{1,0:T(8,128)(2,1)}, u32[]{:S(2)}, u32[]{:S(2)}) %collective-permute-start.27) | collective-permute-done | bytes 786464 | tf_op jit(solution)/shard_map/ppermute | solution.py:300
  137.1 1.1 collective-permute-start.13
  138.3 31.8 %collective-permute-done.18.refs_1_ = bf16[96,4096]{1,0:T(8,128)(2,1)} collective-permute-done((bf16[96,4096]{1,0:T(8,128)(2,1)}, bf16[96,4096]{1,0:T(8,128)(2,1)}, u32[]{:S(2)}, u32[]{:S(2)}) %collective-permute-start.18) | collective-permute-done | bytes 786464 | tf_op jit(solution)/shard_map/ppermute | solution.py:300
  170.2 1.1 copy-done.15
  171.3 1.0 copy-done.23
  172.3 1.0 copy-done.25
  175.3 13.7 %shard_map.200.refs_7_ = f32[8,2,128]{2,1,0:T(2,128)S(1)} custom-call(s32[2,24]{1,0:T(2,128)S(1)} %pad_add_fusion.2.table_ref, bf16[48,4096]{1,0:T(8,128)(2,1)S(1)} %copy-done.23, bf16[48,4096]{1,0:T(8,128)(2,1)S(1)} %copy-done.25, bf16[48,4096]{1,0:T(8,128)(2,1)S(1)} %copy-done.27, bf16[48,4096]{1,0:T(8,128)(2,1)S(1)} %copy-done.29, ...), custom_call_target="tpu_custom_call" | custom-call | flops 5435817984 | bytes 12582912 | tf_op jit(solution)/shard_map/pallas_call | solution.py:157
  189.0 2.6 shard_map.195
  191.6 1.5 collective-permute-start.5
  193.1 3.0 %collective-permute-start.6 = (bf16[48,4096]{1,0:T(8,128)(2,1)S(1)}, bf16[48,4096]{1,0:T(8,128)(2,1)S(1)}, u32[]{:S(2)}, u32[]{:S(2)}) collective-permute-start(bf16[48,4096]{1,0:T(8,128)(2,1)S(1)} %get-tuple-element.29), channel_id=1, source_target_pairs={{0,32},{16,48},{32,0},{48,16},{1,33},{17,49},{33,1},{49,17},{2,34}... | collective-permute-start | bytes 1179656 | tf_op jit(solution)/shard_map/ppermute | solution.py:300
  196.1 7.7 %collective-permute-done.13.refs_1_ = bf16[96,4096]{1,0:T(8,128)(2,1)} collective-permute-done((bf16[96,4096]{1,0:T(8,128)(2,1)}, bf16[96,4096]{1,0:T(8,128)(2,1)}, u32[]{:S(2)}, u32[]{:S(2)}) %collective-permute-start.13) | collective-permute-done | bytes 786464 | tf_op jit(solution)/shard_map/ppermute | solution.py:300
  203.8 10.1 %shard_map.201.refs_7_ = f32[8,2,128]{2,1,0:T(2,128)S(1)} custom-call(s32[2,16]{1,0:T(2,128)S(1)} %get-tuple-element.54.table_ref, bf16[96,4096]{1,0:T(8,128)(2,1)S(1)} %copy-done.17, bf16[96,4096]{1,0:T(8,128)(2,1)} %collective-permute-done.18.refs_1_, bf16[96,4096]{1,0:T(8,128)(2,1)} %collective-permute-done.19.refs_2_, ...), custom_call_target="tpu_custom_call" | custom-call | flops 3623878656 | bytes 12582912 | tf_op jit(solution)/shard_map/pallas_call | solution.py:157
  214.0 9.4 %shard_map.202.refs_7_ = f32[8,2,128]{2,1,0:T(2,128)S(1)} custom-call(s32[2,16]{1,0:T(2,128)S(1)} %get-tuple-element.55.table_ref, bf16[96,4096]{1,0:T(8,128)(2,1)S(1)} %copy-done.19, bf16[96,4096]{1,0:T(8,128)(2,1)} %collective-permute-done.13.refs_1_, bf16[96,4096]{1,0:T(8,128)(2,1)S(1)} %collective-permute-done.14.refs_2_, ...), custom_call_target="tpu_custom_call" | custom-call | flops 3623878656 | bytes 12582912 | tf_op jit(solution)/shard_map/pallas_call | solution.py:157
  223.4 6.2 %shard_map.203 = f32[8,2,128]{2,1,0:T(2,128)S(1)} custom-call(s32[2,8]{1,0:T(2,128)S(1)} %pad.table_ref, bf16[48,4096]{1,0:T(8,128)(2,1)S(1)} %get-tuple-element.27.refs_0_, bf16[48,4096]{1,0:T(8,128)(2,1)S(1)} %collective-permute-done.5.refs_1_, bf16[48,4096]{1,0:T(8,128)(2,1)S(1)} %collective-permute-done.6.refs_2_, ...), custom_call_target="tpu_custom_call" | custom-call | flops 1811939328 | bytes 12582912 | tf_op jit(solution)/shard_map/pallas_call | solution.py:157
  230.3 10.0 %all-to-all-start = ((f32[64,2,128]{2,1,0:T(2,128)}), f32[64,2,128]{2,1,0:T(2,128)S(1)}, u32[]{:S(2)}, u32[]{:S(2)}) async-start(f32[64,2,128]{2,1,0:T(2,128)} %bitcast.13), calls=%async_computation | async-start | bytes 131072 | tf_op jit(solution)/shard_map/all_to_all | solution.py:350
  240.6 4.4 %shard_map.204 = (f32[8,128,64]{2,1,0:T(8,128)S(1)}, f32[8,128,64]{2,1,0:T(8,128)S(1)}, bf16[1024,512]{1,0:T(8,128)(2,1)S(1)}) custom-call(s32[3]{0:T(128)S(1)} %pad_add_fusion.3.here_ref, bf16[128,4224]{1,0:T(8,128)(2,1)S(1)} %shard_map.194.refs_0_, bf16[128,4224]{1,0:T(8,128)(2,1)S(1)} %copy-done.4, ...), custom_call_target="tpu_custom_call" | custom-call | flops 1073741824 | bytes 6291456 | tf_op jit(solution)/shard_map/pallas_call | solution.py:204
  246.7 3.3 %all-to-all-done.back_ref = f32[64,2,128]{2,1,0:T(2,128)S(1)} async-done(((f32[64,2,128]{2,1,0:T(2,128)}), f32[64,2,128]{2,1,0:T(2,128)S(1)}, u32[]{:S(2)}, u32[]{:S(2)}) %all-to-all-start) | async-done | bytes 65568 | tf_op jit(solution)/shard_map/all_to_all | solution.py:350
  250.1 1.2 copy-done.9
  251.3 1.0 copy-done.11
  252.3 4.2 %shard_map.205 = (f32[128,8]{1,0:T(8,128)S(1)}, f32[4,8,16,128]{3,2,1,0:T(8,128)}) custom-call(s32[3]{0:T(128)S(1)} %pad_add_fusion.3.here_ref, f32[64,2,128]{2,1,0:T(2,128)S(1)} %all-to-all-done.back_ref, f32[8,128,64]{2,1,0:T(8,128)S(1)} %get-tuple-element.47.gates_ref, f32[8,128,64]{2,1,0:T(8,128)S(1)} %copy-done.11, bf16[1024,512]{1,0:T(8,128)(2,1)S(1)} %copy-done.9, ...), custom_call_target="tpu_custom_call" | custom-call | flops 268435456 | bytes 3145728 | tf_op jit(solution)/shard_map/pallas_call | solution.py:270
  256.5 5.8 %all-to-all-start.1 = ((f32[32,16,128]{2,1,0:T(8,128)}), f32[32,16,128]{2,1,0:T(8,128)S(1)}, u32[]{:S(2)}, u32[]{:S(2)}) async-start(f32[32,16,128]{2,1,0:T(8,128)} %bitcast.14), calls=%async_computation.1 | async-start | bytes 524288 | tf_op jit(solution)/shard_map/all_to_all | solution.py:353
  262.9 8.3 %all-to-all-done.1.parts_ref = f32[32,16,128]{2,1,0:T(8,128)S(1)} async-done(((f32[32,16,128]{2,1,0:T(8,128)}), f32[32,16,128]{2,1,0:T(8,128)S(1)}, u32[]{:S(2)}, u32[]{:S(2)}) %all-to-all-start.1) | async-done | bytes 262176 | tf_op jit(solution)/shard_map/all_to_all | solution.py:353
  271.9 1.7 shard_map.206
  (134 shorter events, 19.9 us)
Async XLA Ops:
  3.9 30.0 %collective-permute-start = (bf16[128,4224]{1,0:T(8,128)(2,1)S(1)}, bf16[128,4224]{1,0:T(8,128)(2,1)S(1)}, u32[]{:S(2)}, u32[]{:S(2)}) collective-permute-start(bf16[128,4224]{1,0:T(8,128)(2,1)S(1)} %shard_map.194.refs_0_), channel_id=1, source_target_pairs={{0,2},{2,4},{4,6},{6,8},{8,10},{10,12},{12,14},{14,0},{1,3},{3,5},... | collective-permute-start | bytes 3244040 | tf_op jit(solution)/shard_map/ppermute | solution.py:300
  6.4 27.5 %collective-permute-start.8 = (bf16[128,4224]{1,0:T(8,128)(2,1)S(1)}, bf16[128,4224]{1,0:T(8,128)(2,1)S(1)}, u32[]{:S(2)}, u32[]{:S(2)}) collective-permute-start(bf16[128,4224]{1,0:T(8,128)(2,1)S(1)} %shard_map.194.refs_0_), channel_id=1, source_target_pairs={{0,14},{2,0},{4,2},{6,4},{8,6},{10,8},{12,10},{14,12},{1,15},{3,1}... | collective-permute-start | bytes 3244040 | tf_op jit(solution)/shard_map/ppermute | solution.py:300
  10.4 26.2 %collective-permute-start.21 = (bf16[128,4224]{1,0:T(8,128)(2,1)S(1)}, bf16[128,4224]{1,0:T(8,128)(2,1)}, u32[]{:S(2)}, u32[]{:S(2)}) collective-permute-start(bf16[128,4224]{1,0:T(8,128)(2,1)S(1)} %shard_map.194.refs_0_), channel_id=1, source_target_pairs={{0,1},{1,0},{2,3},{3,2},{4,5},{5,4},{6,7},{7,6},{8,9},{9,8},{10,11... | collective-permute-start | bytes 3244040 | tf_op jit(solution)/shard_map/ppermute | solution.py:300
  33.9 58.6 %copy-start.1 = (bf16[128,4224]{1,0:T(8,128)(2,1)}, bf16[128,4224]{1,0:T(8,128)(2,1)S(1)}, u32[]{:S(2)}) copy-start(bf16[128,4224]{1,0:T(8,128)(2,1)S(1)} %collective-permute-done.refs_0_.refs_7_) | copy-start | bytes 3244036
  33.9 25.5 %collective-permute-start.1 = (bf16[128,4224]{1,0:T(8,128)(2,1)S(1)}, bf16[128,4224]{1,0:T(8,128)(2,1)}, u32[]{:S(2)}, u32[]{:S(2)}) collective-permute-start(bf16[128,4224]{1,0:T(8,128)(2,1)S(1)} %collective-permute-done.refs_0_.refs_7_), channel_id=1, source_target_pairs={{0,2},{2,4},{4,6},{6,8},{8,10},{10,12},{12,14},{14,0},{1,3},{3,5},... | collective-permute-start | bytes 3244040 | tf_op jit(solution)/shard_map/ppermute | solution.py:300
  33.9 25.5 %copy-start.2 = (bf16[128,4224]{1,0:T(8,128)(2,1)}, bf16[128,4224]{1,0:T(8,128)(2,1)S(1)}, u32[]{:S(2)}) copy-start(bf16[128,4224]{1,0:T(8,128)(2,1)S(1)} %collective-permute-done.8.refs_1_) | copy-start | bytes 3244036
  33.9 31.2 %collective-permute-start.9 = (bf16[128,4224]{1,0:T(8,128)(2,1)S(1)}, bf16[128,4224]{1,0:T(8,128)(2,1)}, u32[]{:S(2)}, u32[]{:S(2)}) collective-permute-start(bf16[128,4224]{1,0:T(8,128)(2,1)S(1)} %collective-permute-done.8.refs_1_), channel_id=1, source_target_pairs={{0,14},{2,0},{4,2},{6,4},{8,6},{10,8},{12,10},{14,12},{1,15},{3,1}... | collective-permute-start | bytes 3244040 | tf_op jit(solution)/shard_map/ppermute | solution.py:300
  39.9 21.6 %collective-permute-start.22 = (bf16[48,4096]{1,0:T(8,128)(2,1)S(1)}, bf16[48,4096]{1,0:T(8,128)(2,1)S(1)}, u32[]{:S(2)}, u32[]{:S(2)}) collective-permute-start(bf16[48,4096]{1,0:T(8,128)(2,1)S(1)} %get-tuple-element.40), channel_id=1, source_target_pairs={{0,16},{16,32},{32,48},{48,0},{1,17},{17,33},{33,49},{49,1},{2,18}... | collective-permute-start | bytes 1179656 | tf_op jit(solution)/shard_map/ppermute | solution.py:300
  41.2 46.8 %collective-permute-start.25 = (bf16[128,4224]{1,0:T(8,128)(2,1)S(1)}, bf16[128,4224]{1,0:T(8,128)(2,1)S(1)}, u32[]{:S(2)}, u32[]{:S(2)}) collective-permute-start(bf16[128,4224]{1,0:T(8,128)(2,1)S(1)} %collective-permute-done.refs_0_.refs_7_), channel_id=1, source_target_pairs={{0,1},{1,0},{2,3},{3,2},{4,5},{5,4},{6,7},{7,6},{8,9},{9,8},{10,11... | collective-permute-start | bytes 3244040 | tf_op jit(solution)/shard_map/ppermute | solution.py:300
  59.3 28.7 %collective-permute-start.2 = (bf16[128,4224]{1,0:T(8,128)(2,1)}, bf16[128,4224]{1,0:T(8,128)(2,1)S(1)}, u32[]{:S(2)}, u32[]{:S(2)}) collective-permute-start(bf16[128,4224]{1,0:T(8,128)(2,1)} %collective-permute-done.1.refs_0_.refs_6_), channel_id=1, source_target_pairs={{0,2},{2,4},{4,6},{6,8},{8,10},{10,12},{12,14},{14,0},{1,3},{3,5},... | collective-permute-start | bytes 3244040 | tf_op jit(solution)/shard_map/ppermute | solution.py:300
  59.4 29.1 %collective-permute-start.26 = (bf16[128,4224]{1,0:T(8,128)(2,1)S(1)}, bf16[128,4224]{1,0:T(8,128)(2,1)S(1)}, u32[]{:S(2)}, u32[]{:S(2)}) collective-permute-start(bf16[128,4224]{1,0:T(8,128)(2,1)S(1)} %collective-permute-done.8.refs_1_), channel_id=1, source_target_pairs={{0,1},{1,0},{2,3},{3,2},{4,5},{5,4},{6,7},{7,6},{8,9},{9,8},{10,11... | collective-permute-start | bytes 3244040 | tf_op jit(solution)/shard_map/ppermute | solution.py:300
  62.2 12.2 %collective-permute-start.23 = (bf16[48,4096]{1,0:T(8,128)(2,1)S(1)}, bf16[48,4096]{1,0:T(8,128)(2,1)S(1)}, u32[]{:S(2)}, u32[]{:S(2)}) collective-permute-start(bf16[48,4096]{1,0:T(8,128)(2,1)S(1)} %get-tuple-element.41), channel_id=1, source_target_pairs={{0,32},{16,48},{32,0},{48,16},{1,33},{17,49},{33,1},{49,17},{2,34}... | collective-permute-start | bytes 1179656 | tf_op jit(solution)/shard_map/ppermute | solution.py:300
  65.1 26.2 %collective-permute-start.10 = (bf16[128,4224]{1,0:T(8,128)(2,1)}, bf16[128,4224]{1,0:T(8,128)(2,1)}, u32[]{:S(2)}, u32[]{:S(2)}) collective-permute-start(bf16[128,4224]{1,0:T(8,128)(2,1)} %collective-permute-done.9.refs_1_.refs_2_), channel_id=1, source_target_pairs={{0,14},{2,0},{4,2},{6,4},{8,6},{10,8},{12,10},{14,12},{1,15},{3,1}... | collective-permute-start | bytes 3244040 | tf_op jit(solution)/shard_map/ppermute | solution.py:300
  75.1 41.2 %copy-start.41 = (s32[16]{0:T(128)S(1)}, s32[16]{0:T(128)}, u32[]{:S(2)}) copy-start(s32[16]{0:T(128)} %constant.132.clone) | copy-start | bytes 196
  75.1 41.2 %copy-start.42 = (s32[16]{0:T(128)S(1)}, s32[16]{0:T(128)}, u32[]{:S(2)}) copy-start(s32[16]{0:T(128)} %constant.133.clone) | copy-start | bytes 196
  75.1 10.3 %collective-permute-start.24 = (bf16[48,4096]{1,0:T(8,128)(2,1)S(1)}, bf16[48,4096]{1,0:T(8,128)(2,1)S(1)}, u32[]{:S(2)}, u32[]{:S(2)}) collective-permute-start(bf16[48,4096]{1,0:T(8,128)(2,1)S(1)} %get-tuple-element.42), channel_id=1, source_target_pairs={{0,48},{16,0},{32,16},{48,32},{1,49},{17,1},{33,17},{49,33},{2,50}... | collective-permute-start | bytes 1179656 | tf_op jit(solution)/shard_map/ppermute | solution.py:300
  86.2 13.0 %collective-permute-start.16 = (bf16[128,4224]{1,0:T(8,128)(2,1)}, bf16[128,4224]{1,0:T(8,128)(2,1)S(1)}, u32[]{:S(2)}, u32[]{:S(2)}) collective-permute-start(bf16[128,4224]{1,0:T(8,128)(2,1)} %collective-permute-done.1.refs_0_.refs_6_), channel_id=1, source_target_pairs={{0,1},{1,0},{2,3},{3,2},{4,5},{5,4},{6,7},{7,6},{8,9},{9,8},{10,11... | collective-permute-start | bytes 3244040 | tf_op jit(solution)/shard_map/ppermute | solution.py:300
  88.0 11.7 %collective-permute-start.17 = (bf16[128,4224]{1,0:T(8,128)(2,1)}, bf16[128,4224]{1,0:T(8,128)(2,1)S(1)}, u32[]{:S(2)}, u32[]{:S(2)}) collective-permute-start(bf16[128,4224]{1,0:T(8,128)(2,1)} %collective-permute-done.9.refs_1_.refs_2_), channel_id=1, source_target_pairs={{0,1},{1,0},{2,3},{3,2},{4,5},{5,4},{6,7},{7,6},{8,9},{9,8},{10,11... | collective-permute-start | bytes 3244040 | tf_op jit(solution)/shard_map/ppermute | solution.py:300
  88.1 10.3 %copy-start.5 = (bf16[128,4224]{1,0:T(8,128)(2,1)}, bf16[128,4224]{1,0:T(8,128)(2,1)S(1)}, u32[]{:S(2)}) copy-start(bf16[128,4224]{1,0:T(8,128)(2,1)S(1)} %collective-permute-done.2.refs_0_.refs_5_) | copy-start | bytes 3244036
  88.1 13.2 %collective-permute-start.11 = (bf16[128,4224]{1,0:T(8,128)(2,1)S(1)}, bf16[128,4224]{1,0:T(8,128)(2,1)S(1)}, u32[]{:S(2)}, u32[]{:S(2)}) collective-permute-start(bf16[128,4224]{1,0:T(8,128)(2,1)S(1)} %collective-permute-done.2.refs_0_.refs_5_), channel_id=1, source_target_pairs={{0,1},{1,0},{2,3},{3,2},{4,5},{5,4},{6,7},{7,6},{8,9},{9,8},{10,11... | collective-permute-start | bytes 3244040 | tf_op jit(solution)/shard_map/ppermute | solution.py:300
  88.5 27.2 %collective-permute-start.3 = (bf16[128,4224]{1,0:T(8,128)(2,1)S(1)}, bf16[128,4224]{1,0:T(8,128)(2,1)S(1)}, u32[]{:S(2)}, u32[]{:S(2)}) collective-permute-start(bf16[128,4224]{1,0:T(8,128)(2,1)S(1)} %collective-permute-done.2.refs_0_.refs_5_), channel_id=1, source_target_pairs={{0,2},{2,4},{4,6},{6,8},{8,10},{10,12},{12,14},{14,0},{1,3},{3,5},... | collective-permute-start | bytes 3244040 | tf_op jit(solution)/shard_map/ppermute | solution.py:300
  91.3 31.4 %collective-permute-start.12 = (bf16[128,4224]{1,0:T(8,128)(2,1)}, bf16[128,4224]{1,0:T(8,128)(2,1)}, u32[]{:S(2)}, u32[]{:S(2)}) collective-permute-start(bf16[128,4224]{1,0:T(8,128)(2,1)} %collective-permute-done.10.refs_1_.refs_3_), channel_id=1, source_target_pairs={{0,1},{1,0},{2,3},{3,2},{4,5},{5,4},{6,7},{7,6},{8,9},{9,8},{10,11... | collective-permute-start | bytes 3244040 | tf_op jit(solution)/shard_map/ppermute | solution.py:300
  99.3 17.0 %copy-start.32 = (bf16[128,4224]{1,0:T(8,128)(2,1)}, bf16[128,4224]{1,0:T(8,128)(2,1)S(1)}, u32[]{:S(2)}) copy-start(bf16[128,4224]{1,0:T(8,128)(2,1)S(1)} %collective-permute-done.16.refs_2_) | copy-start | bytes 3244036
  99.3 37.2 %collective-permute-start.27 = (bf16[96,4096]{1,0:T(8,128)(2,1)}, bf16[96,4096]{1,0:T(8,128)(2,1)}, u32[]{:S(2)}, u32[]{:S(2)}) collective-permute-start(bf16[96,4096]{1,0:T(8,128)(2,1)} %get-tuple-element.44), channel_id=1, source_target_pairs={{0,16},{16,32},{32,48},{48,0},{1,17},{17,33},{33,49},{49,1},{2,18}... | collective-permute-start | bytes 2359304 | tf_op jit(solution)/shard_map/ppermute | solution.py:300
  99.7 16.6 %copy-start.33 = (bf16[128,4224]{1,0:T(8,128)(2,1)}, bf16[128,4224]{1,0:T(8,128)(2,1)S(1)}, u32[]{:S(2)}) copy-start(bf16[128,4224]{1,0:T(8,128)(2,1)S(1)} %collective-permute-done.17.refs_3_) | copy-start | bytes 3244036
  99.7 36.8 %collective-permute-start.28 = (bf16[96,4096]{1,0:T(8,128)(2,1)}, bf16[96,4096]{1,0:T(8,128)(2,1)}, u32[]{:S(2)}, u32[]{:S(2)}) collective-permute-start(bf16[96,4096]{1,0:T(8,128)(2,1)} %get-tuple-element.45), channel_id=1, source_target_pairs={{0,32},{16,48},{32,0},{48,16},{1,33},{17,49},{33,1},{49,17},{2,34}... | collective-permute-start | bytes 2359304 | tf_op jit(solution)/shard_map/ppermute | solution.py:300
  101.2 14.4 %copy-start.30 = (bf16[128,4224]{1,0:T(8,128)(2,1)}, bf16[128,4224]{1,0:T(8,128)(2,1)S(1)}, u32[]{:S(2)}) copy-start(bf16[128,4224]{1,0:T(8,128)(2,1)S(1)} %collective-permute-done.11.refs_2_) | copy-start | bytes 3244036
  101.3 35.9 %collective-permute-start.29 = (bf16[96,4096]{1,0:T(8,128)(2,1)}, bf16[96,4096]{1,0:T(8,128)(2,1)}, u32[]{:S(2)}, u32[]{:S(2)}) collective-permute-start(bf16[96,4096]{1,0:T(8,128)(2,1)} %get-tuple-element.46), channel_id=1, source_target_pairs={{0,48},{16,0},{32,16},{48,32},{1,49},{17,1},{33,17},{49,33},{2,50}... | collective-permute-start | bytes 2359304 | tf_op jit(solution)/shard_map/ppermute | solution.py:300
  115.7 73.3 %copy-start = (bf16[128,4224]{1,0:T(8,128)(2,1)}, bf16[128,4224]{1,0:T(8,128)(2,1)S(1)}, u32[]{:S(2)}) copy-start(bf16[128,4224]{1,0:T(8,128)(2,1)S(1)} %collective-permute-done.3.refs_0_.refs_4_) | copy-start | bytes 3244036
  115.7 54.4 %collective-permute-start.4 = (bf16[128,4224]{1,0:T(8,128)(2,1)S(1)}, bf16[128,4224]{1,0:T(8,128)(2,1)}, u32[]{:S(2)}, u32[]{:S(2)}) collective-permute-start(bf16[128,4224]{1,0:T(8,128)(2,1)S(1)} %collective-permute-done.3.refs_0_.refs_4_), channel_id=1, source_target_pairs={{0,1},{1,0},{2,3},{3,2},{4,5},{5,4},{6,7},{7,6},{8,9},{9,8},{10,11... | collective-permute-start | bytes 3244040 | tf_op jit(solution)/shard_map/ppermute | solution.py:300
  122.7 47.4 %collective-permute-start.18 = (bf16[96,4096]{1,0:T(8,128)(2,1)}, bf16[96,4096]{1,0:T(8,128)(2,1)}, u32[]{:S(2)}, u32[]{:S(2)}) collective-permute-start(bf16[96,4096]{1,0:T(8,128)(2,1)} %get-tuple-element.36), channel_id=1, source_target_pairs={{0,16},{16,32},{32,48},{48,0},{1,17},{17,33},{33,49},{49,1},{2,18}... | collective-permute-start | bytes 2359304 | tf_op jit(solution)/shard_map/ppermute | solution.py:300
  123.7 14.6 %copy-start.37 = (s32[8]{0:T(128)S(1)}, s32[8]{0:T(128)}, u32[]{:S(2)}) copy-start(s32[8]{0:T(128)} %constant.135.clone) | copy-start | bytes 100
  123.7 14.6 %copy-start.38 = (s32[8]{0:T(128)S(1)}, s32[8]{0:T(128)}, u32[]{:S(2)}) copy-start(s32[8]{0:T(128)} %constant.143) | copy-start | bytes 100
  136.5 55.2 %collective-permute-start.19 = (bf16[96,4096]{1,0:T(8,128)(2,1)}, bf16[96,4096]{1,0:T(8,128)(2,1)}, u32[]{:S(2)}, u32[]{:S(2)}) collective-permute-start(bf16[96,4096]{1,0:T(8,128)(2,1)} %get-tuple-element.37), channel_id=1, source_target_pairs={{0,32},{16,48},{32,0},{48,16},{1,33},{17,49},{33,1},{49,17},{2,34}... | collective-permute-start | bytes 2359304 | tf_op jit(solution)/shard_map/ppermute | solution.py:300
  136.5 56.7 %collective-permute-start.20 = (bf16[96,4096]{1,0:T(8,128)(2,1)}, bf16[96,4096]{1,0:T(8,128)(2,1)}, u32[]{:S(2)}, u32[]{:S(2)}) collective-permute-start(bf16[96,4096]{1,0:T(8,128)(2,1)} %get-tuple-element.38), channel_id=1, source_target_pairs={{0,48},{16,0},{32,16},{48,32},{1,49},{17,1},{33,17},{49,33},{2,50}... | collective-permute-start | bytes 2359304 | tf_op jit(solution)/shard_map/ppermute | solution.py:300
  137.1 66.7 %collective-permute-start.13 = (bf16[96,4096]{1,0:T(8,128)(2,1)}, bf16[96,4096]{1,0:T(8,128)(2,1)}, u32[]{:S(2)}, u32[]{:S(2)}) collective-permute-start(bf16[96,4096]{1,0:T(8,128)(2,1)} %get-tuple-element.32), channel_id=1, source_target_pairs={{0,16},{16,32},{32,48},{48,0},{1,17},{17,33},{33,49},{49,1},{2,18}... | collective-permute-start | bytes 2359304 | tf_op jit(solution)/shard_map/ppermute | solution.py:300
  170.1 43.8 %collective-permute-start.14 = (bf16[96,4096]{1,0:T(8,128)(2,1)}, bf16[96,4096]{1,0:T(8,128)(2,1)S(1)}, u32[]{:S(2)}, u32[]{:S(2)}) collective-permute-start(bf16[96,4096]{1,0:T(8,128)(2,1)} %copy-done.21), channel_id=1, source_target_pairs={{0,32},{16,48},{32,0},{48,16},{1,33},{17,49},{33,1},{49,17},{2,34}... | collective-permute-start | bytes 2359304 | tf_op jit(solution)/shard_map/ppermute | solution.py:300
  170.1 43.8 %collective-permute-start.15 = (bf16[96,4096]{1,0:T(8,128)(2,1)}, bf16[96,4096]{1,0:T(8,128)(2,1)S(1)}, u32[]{:S(2)}, u32[]{:S(2)}) collective-permute-start(bf16[96,4096]{1,0:T(8,128)(2,1)} %copy-done.20), channel_id=1, source_target_pairs={{0,48},{16,0},{32,16},{48,32},{1,49},{17,1},{33,17},{49,33},{2,50}... | collective-permute-start | bytes 2359304 | tf_op jit(solution)/shard_map/ppermute | solution.py:300
  189.0 14.8 %copy-start.17 = (bf16[96,4096]{1,0:T(8,128)(2,1)S(1)}, bf16[96,4096]{1,0:T(8,128)(2,1)}, u32[]{:S(2)}) copy-start(bf16[96,4096]{1,0:T(8,128)(2,1)} %copy-done.16) | copy-start | bytes 2359300
  191.6 31.7 %collective-permute-start.5 = (bf16[48,4096]{1,0:T(8,128)(2,1)S(1)}, bf16[48,4096]{1,0:T(8,128)(2,1)S(1)}, u32[]{:S(2)}, u32[]{:S(2)}) collective-permute-start(bf16[48,4096]{1,0:T(8,128)(2,1)S(1)} %get-tuple-element.28), channel_id=1, source_target_pairs={{0,16},{16,32},{32,48},{48,0},{1,17},{17,33},{33,49},{49,1},{2,18}... | collective-permute-start | bytes 1179656 | tf_op jit(solution)/shard_map/ppermute | solution.py:300
  193.1 30.2 %collective-permute-start.6 = (bf16[48,4096]{1,0:T(8,128)(2,1)S(1)}, bf16[48,4096]{1,0:T(8,128)(2,1)S(1)}, u32[]{:S(2)}, u32[]{:S(2)}) collective-permute-start(bf16[48,4096]{1,0:T(8,128)(2,1)S(1)} %get-tuple-element.29), channel_id=1, source_target_pairs={{0,32},{16,48},{32,0},{48,16},{1,33},{17,49},{33,1},{49,17},{2,34}... | collective-permute-start | bytes 1179656 | tf_op jit(solution)/shard_map/ppermute | solution.py:300
  203.8 19.6 %collective-permute-start.7 = (bf16[48,4096]{1,0:T(8,128)(2,1)S(1)}, bf16[48,4096]{1,0:T(8,128)(2,1)S(1)}, u32[]{:S(2)}, u32[]{:S(2)}) collective-permute-start(bf16[48,4096]{1,0:T(8,128)(2,1)S(1)} %get-tuple-element.30), channel_id=1, source_target_pairs={{0,48},{16,0},{32,16},{48,32},{1,49},{17,1},{33,17},{49,33},{2,50}... | collective-permute-start | bytes 1179656 | tf_op jit(solution)/shard_map/ppermute | solution.py:300
  203.8 10.1 %copy-start.19 = (bf16[96,4096]{1,0:T(8,128)(2,1)S(1)}, bf16[96,4096]{1,0:T(8,128)(2,1)}, u32[]{:S(2)}) copy-start(bf16[96,4096]{1,0:T(8,128)(2,1)} %copy-done.18) | copy-start | bytes 2359300
  214.0 9.4 %copy-start.7 = (bf16[1,2048,768]{2,1,0:T(8,128)(2,1)S(1)}, bf16[1,2048,768]{2,1,0:T(8,128)(2,1)}, u32[]{:S(2)}) copy-start(bf16[1,2048,768]{2,1,0:T(8,128)(2,1)} %param.23) | copy-start | bytes 9437188
  223.4 16.9 %copy-start.36 = (bf16[2048,64]{0,1:T(8,128)(2,1)S(1)}, bf16[2048,64]{0,1:T(8,128)(2,1)}, u32[]{:S(2)}) copy-start(bf16[2048,64]{0,1:T(8,128)(2,1)} %param.21) | copy-start | bytes 786436
  223.4 17.1 %copy-start.4 = (bf16[128,4224]{1,0:T(8,128)(2,1)S(1)}, bf16[128,4224]{1,0:T(8,128)(2,1)}, u32[]{:S(2)}) copy-start(bf16[128,4224]{1,0:T(8,128)(2,1)} %copy-done.2) | copy-start | bytes 3244036
  230.3 19.8 %all-to-all-start = ((f32[64,2,128]{2,1,0:T(2,128)}), f32[64,2,128]{2,1,0:T(2,128)S(1)}, u32[]{:S(2)}, u32[]{:S(2)}) async-start(f32[64,2,128]{2,1,0:T(2,128)} %bitcast.13), calls=%async_computation | async-start | bytes 131072 | tf_op jit(solution)/shard_map/all_to_all | solution.py:350
  256.5 14.7 %all-to-all-start.1 = ((f32[32,16,128]{2,1,0:T(8,128)}), f32[32,16,128]{2,1,0:T(8,128)S(1)}, u32[]{:S(2)}, u32[]{:S(2)}) async-start(f32[32,16,128]{2,1,0:T(8,128)} %bitcast.14), calls=%async_computation.1 | async-start | bytes 524288 | tf_op jit(solution)/shard_map/all_to_all | solution.py:353
  (30 other events, 72.8 us)
where the time goes:
time: 274 us
  waiting for transfers between devices  126 us (46%)
  Pallas kernels  69.7 us (25%)
  starting transfers between devices  53.4 us (19%)
  local copies, waits for them, and re-layouts  23.1 us (8%)
    ppermute x30, waiting for transfers between devices, shifted(): lax.ppermute(array, axis, [(i, (i + by) % size) for i in range(size)])  114 us
    pallas_call x4, Pallas kernels, expert(): pl.pallas_call(functools.partial(expert_kernel, steps, chunk), grid=(step...  39.4 us
    ppermute x30, starting transfers between devices, shifted(): lax.ppermute(array, axis, [(i, (i + by) % size) for i in range(size)])  37.6 us
    unnamed x95, local copies, waits for them, and re-layouts  22.5 us
    pallas_call x5, Pallas kernels, pick(): pl.pallas_call(functools.partial(pick_kernel, count), out_shape=[jax.Shap...  19.7 us
    all_to_all x1, starting transfers between devices, on_device(): back = lax.all_to_all(back, ('y', 'z', 'c'), 0, 0, tiled=True)  10 us
    all_to_all x1, waiting for transfers between devices, on_device(): lax.all_to_all(part.reshape(copies * NY * NC, 16, 2 * experts), ('dp', 'y...  8.3 us
    all_to_all x1, starting transfers between devices, on_device(): lax.all_to_all(part.reshape(copies * NY * NC, 16, 2 * experts), ('dp', 'y...  5.76 us
  transfers between devices with their start and end apart: 32, of which 12 were waited for; matrix products, arithmetic and copies ran while one was open for 0% of the time, Pallas kernels for 21%

commit v1 on v0

--- a/solution.py
+++ b/solution.py
@@ -12,7 +12,7 @@
 NY, NZ, NC = 4, 8, 2
 CAP = 24
 PACK, STRIDE = 4, 32
-VMEM = 48 * 1024 * 1024
+VMEM = 32 * 1024 * 1024
 
 
 def params():
@@ -21,6 +21,10 @@
 
 def in_vmem(count):
     return [pl.BlockSpec(memory_space=pltpu.VMEM)] * count
+
+
+def in_hbm(array):
+    return pltpu.with_memory_space_constraint(array, pltpu.HBM)
 
 
 def in_smem():
@@ -31,10 +35,11 @@
     rows, width = tok_ref.shape
     out_ref[:, :width] = tok_ref[...]
     out_ref[:, width : 2 * width] = grad_ref[...]
-    lane = lax.broadcasted_iota(jnp.int32, (rows, 128), 1)
-    hit = jnp.zeros((rows, 128), jnp.float32)
-    for k in range(idx_ref.shape[1]):
-        hit = hit + (idx_ref[:, k : k + 1] == lane).astype(jnp.float32)
+    label = lax.broadcasted_iota(jnp.int32, (128, rows), 0)
+    hit = jnp.zeros((128, rows), jnp.float32)
+    for k in range(idx_ref.shape[0]):
+        hit = hit + (idx_ref[k : k + 1, :] == label).astype(jnp.float32)
+    hit = hit.T
     earlier = lax.broadcasted_iota(jnp.int32, (rows, rows), 0) > lax.broadcasted_iota(
         jnp.int32, (rows, rows), 1
     )
@@ -71,14 +76,16 @@
     @pl.loop(0, width // tile)
     def _(step):
         cols = pl.ds(pl.multiple_of(step * tile, tile), tile)
-        for i in range(count):
-            taken = jnp.dot(
-                chosen_ref[i], slices[i][:, cols], preferred_element_type=jnp.float32
-            )
+        for i in range(0, count, 2):
+            taken = [
+                jnp.dot(chosen_ref[j], slices[j][:, cols], preferred_element_type=jnp.float32)
+                for j in (i, i + 1)
+            ]
             for dy in range(NY):
-                outs[dy][i * CAP : (i + 1) * CAP, cols] = taken[
-                    dy * CAP : (dy + 1) * CAP
-                ].astype(jnp.bfloat16)
+                both = [t[dy * CAP : (dy + 1) * CAP] for t in taken]
+                outs[dy][i * CAP : (i + 2) * CAP, cols] = jnp.concatenate(both, axis=0).astype(
+                    jnp.bfloat16
+                )
 
 
 def pick(here, slices):
@@ -86,7 +93,8 @@
     rows, width = slices[0].shape[0], slices[0].shape[1] - 128
     return pl.pallas_call(
         functools.partial(pick_kernel, count),
-        out_shape=[jax.ShapeDtypeStruct((count * CAP, width), jnp.bfloat16)] * NY,
+        out_shape=[pltpu.HBM((count * CAP, width), jnp.bfloat16)]
+        + [jax.ShapeDtypeStruct((count * CAP, width), jnp.bfloat16)] * (NY - 1),
         in_specs=in_smem() + in_vmem(count),
         out_specs=in_vmem(NY),
         scratch_shapes=[pltpu.VMEM((count, NY * CAP, rows), jnp.bfloat16)],
@@ -148,12 +156,12 @@
                 out_ref[home, pl.ds(source // PACK, 1), :] += line
 
 
-def expert(table, parts, gate_w, up_w, down_w, before):
+def expert(table, parts, gate_w, up_w, down_w, before, final):
     width, inner = gate_w.shape
     tile = 256
     steps = inner // tile
     rows = sum(part.shape[0] for part in parts)
-    chunk = rows if rows <= 384 else rows // 2
+    chunk = rows if final else 192
     return pl.pallas_call(
         functools.partial(expert_kernel, steps, chunk),
         grid=(steps,),
@@ -179,14 +187,14 @@
     )(table, *parts, gate_w, up_w, down_w, before)
 
 
-def side_kernel(here_ref, *refs):
+def side_kernel(keys, here_ref, *refs):
     slices, router_ref, gates_ref, place_ref, feats_ref = refs[:NZ], *refs[NZ:]
-    z = here_ref[1]
+    z, c = here_ref[1], here_ref[2]
     rows = slices[0].shape[0]
     width, experts = router_ref.shape
     router = router_ref[...]
     for j in range(NZ):
-        source = (z + j) % NZ
+        source = stop(z, c, *keys[j])
         place = slices[j][:, 2 * width :].astype(jnp.float32)[:, :experts]
         logits = jnp.dot(slices[j][:, :width], router, preferred_element_type=jnp.float32)
         hit = place >= 0.0
@@ -199,10 +207,10 @@
             feats_ref[pl.ds(at, rows), y * 128 : (y + 1) * 128] = slices[j][:, pl.ds(col, 128)]
 
 
-def side(here, slices, router_weight):
+def side(here, keys, slices, router_weight):
     rows, experts = slices[0].shape[0], router_weight.shape[1]
     return pl.pallas_call(
-        side_kernel,
+        functools.partial(side_kernel, keys),
         out_shape=[
             jax.ShapeDtypeStruct((NZ, rows, experts), jnp.float32),
             jax.ShapeDtypeStruct((NZ, rows, experts), jnp.float32),
@@ -218,8 +226,8 @@
 
 
 def finish_kernel(
-    here_ref, back_ref, gates_ref, place_ref, feats_ref, idx_ref,
-    grad_ref, part_ref, table_ref, wide_ref, dense_ref, sum_ref,
+    here_ref, back_ref, gates_ref, place_ref, feats_ref,
+    own_ref, part_ref, table_ref, wide_ref, dense_ref, sum_ref,
 ):
     z = here_ref[1]
     rows, experts = gates_ref.shape[1:]
@@ -253,27 +261,27 @@
             for copy in range(part_ref.shape[0]):
                 part_ref[copy, y * NC + c, :, :experts] = sum_ref[pl.ds(at, half), :]
                 part_ref[copy, y * NC + c, :, experts:] = sum_ref[pl.ds(at + half, half), :]
-    own = wide_ref[z]
-    number = lax.broadcasted_iota(jnp.int32, (rows, experts), 1)
-    lane = lax.broadcasted_iota(jnp.int32, grad_ref.shape, 1)
-    out = jnp.zeros(grad_ref.shape, jnp.float32)
-    for k in range(grad_ref.shape[1]):
-        here_k = idx_ref[:, k : k + 1] == number
-        value = jnp.sum(jnp.where(here_k, own, 0.0), axis=1, keepdims=True)
-        out = jnp.where(lane == k, value, out)
-    grad_ref[...] = out
-
-
-def finish(here, back, gates, place, feats, expert_index, copies):
-    rows, top = expert_index.shape
-    experts = gates.shape[2]
+    own_ref[...] = wide_ref[z]
+
+
+def gate_kernel(own_ref, idx_ref, grad_ref):
+    rows, experts = own_ref.shape
+    number = lax.broadcasted_iota(jnp.int32, (experts, rows), 0)
+    own = own_ref[...].T
+    for k in range(grad_ref.shape[0]):
+        here_k = idx_ref[k : k + 1, :] == number
+        grad_ref[k : k + 1, :] = jnp.sum(jnp.where(here_k, own, 0.0), axis=0, keepdims=True)
+
+
+def finish(here, back, gates, place, feats, copies):
+    rows, experts = gates.shape[1:]
     return pl.pallas_call(
         finish_kernel,
         out_shape=[
-            jax.ShapeDtypeStruct((rows, top), jnp.float32),
+            jax.ShapeDtypeStruct((rows, experts), jnp.float32),
             jax.ShapeDtypeStruct((copies, NY * NC, 16, 2 * experts), jnp.float32),
         ],
-        in_specs=in_smem() + in_vmem(5),
+        in_specs=in_smem() + in_vmem(4),
         out_specs=in_vmem(2),
         scratch_shapes=[
             pltpu.VMEM((NZ * STRIDE, experts), jnp.float32),
@@ -283,7 +291,7 @@
         ],
         compiler_params=params(),
         cost_estimate=pl.CostEstimate(flops=1 << 28, bytes_accessed=3 << 20, transcendentals=0),
-    )(here, back, gates, place, feats, expert_index)
+    )(here, back, gates, place, feats)
 
 
 def sum_kernel(parts_ref, out_ref):
@@ -298,6 +306,18 @@
 def shifted(array, axis, by):
     size = lax.axis_size(axis)
     return lax.ppermute(array, axis, [(i, (i + by) % size) for i in range(size)])
+
+
+def stop(z, core, hops, way):
+    return (z + NZ + hops * (1 - 2 * core) * (2 * way - 1)) % NZ
+
+
+def along_ring(array, way):
+    up = (1 - 2 * way, 2 * way - 1)
+    pairs = [
+        (z * NC + c, (z + up[c]) % NZ * NC + c) for z in range(NZ) for c in range(NC)
+    ]
+    return lax.ppermute(array, ("z", "c"), pairs)
 
 
 def on_device(tokens, grad_out, router_weight, expert_index, w_gate, w_up, w_down):
@@ -309,47 +329,47 @@
         pack_kernel,
         out_shape=jax.ShapeDtypeStruct((tok_rows, 2 * width + 128), jnp.bfloat16),
         compiler_params=params(),
-    )(tokens, grad_out, expert_index)
+    )(in_hbm(tokens), in_hbm(grad_out), expert_index.T)
 
     last = NZ // 2
-    ups, downs = {0: packed}, {0: packed}
+    ring = {(0, way): packed for way in range(2)}
     for step in range(1, last + 1):
-        ups[step] = shifted(ups[step - 1], "z", 1)
-        if step < last:
-            downs[step] = shifted(downs[step - 1], "z", -1)
-    stops, arrived = [], []
-    for step in range(last + 1):
-        if step == 0 or step == last:
-            stops.append((step,))
-            slices = [ups[step]]
-        else:
-            stops.append((NZ - step, step))
-            slices = [ups[step], downs[step]]
+        for way in range(2 if step < last else 1):
+            ring[step, way] = along_ring(ring[step - 1, way], way)
+    groups = [[(0, 0)], [(1, 0)], [(1, 1)]]
+    groups += [[(step, 0), (step, 1)] for step in range(2, last)] + [[(last, 0)]]
+    arrived = []
+    for group in groups:
+        slices = [ring[key] for key in group]
         slices = slices + [shifted(a, "c", 1) for a in slices]
         rows = pick(here, slices)
         arrived.append([rows[0]] + [shifted(rows[dy], "y", dy) for dy in range(1, NY)])
 
     products = jnp.zeros((NY * NC, NZ // PACK, 128), jnp.float32)
-    for steps in ((0, 1), (2,), (3,), (4,)):
+    for i, members in enumerate(((0, 1, 2), (3,), (4,), (5,))):
         parts, table = [], []
-        for step in steps:
+        for g in members:
             for dy in range(NY):
-                parts.append(arrived[step][dy])
-                for core in range(NC):
-                    for offset in stops[step]:
-                        table.append((dy, core, offset))
-        dys, cores, offsets = np.array(table, np.int32).T
-        homes = jnp.stack([(y + NY - dys) % NY * NC + (c + cores) % NC, (z + offsets) % NZ])
-        products = expert(homes, parts, w_gate[0], w_up[0], w_down[0], products)
-    columns = [ups[0]] + [downs[j] for j in range(1, last)] + [ups[last]]
-    columns += [ups[j] for j in range(last - 1, 0, -1)]
-    gates, place, feats = side(here, columns, router_weight)
+                parts.append(arrived[g][dy])
+                table += [(dy, core, *key) for core in range(NC) for key in groups[g]]
+        dy, core, hops, way = np.array(table, np.int32).T
+        core = (c + core) % NC
+        homes = jnp.stack([(y + NY - dy) % NY * NC + core, stop(z, core, hops, way)])
+        final = i == 3
+        weights = [w if final else in_hbm(w) for w in (w_gate[0], w_up[0], w_down[0])]
+        products = expert(homes, parts, *weights, products, final)
+    gates, place, feats = side(here, list(ring)[1:], list(ring.values())[1:], router_weight)
 
     back = products.reshape(NY, 1, NC, NZ // PACK, 128)
     back = jnp.broadcast_to(back, (NY, NZ, NC, NZ // PACK, 128)).reshape(experts, NZ // PACK, 128)
     back = lax.all_to_all(back, ("y", "z", "c"), 0, 0, tiled=True)
     copies = lax.axis_size("dp")
-    gate_grad, part = finish(here, back, gates, place, feats, expert_index, copies)
+    wide, part = finish(here, back, gates, place, feats, copies)
+    gate_grad = pl.pallas_call(
+        gate_kernel,
+        out_shape=jax.ShapeDtypeStruct(expert_index.T.shape, jnp.float32),
+        cost_estimate=pl.CostEstimate(flops=1 << 20, bytes_accessed=1 << 16, transcendentals=0),
+    )(wide, expert_index.T).T
     parts = lax.all_to_all(
         part.reshape(copies * NY * NC, 16, 2 * experts), ("dp", "y", "c"), 0, 0, tiled=True
     )

time: 274 us -> 277 us (1.011)
  starting transfers between devices: 53.4 us -> 79.9 us
  waiting for transfers between devices: 126 us -> 106 us
  local copies, waits for them, and re-layouts: 23.1 us -> 17 us
  Pallas kernels: 69.7 us -> 72.6 us
    ppermute x30 -> x26, waiting for transfers between devices: 114 us -> 62.3 us  [shifted(): lax.ppermute(array, axis, [(i, (i + by) % size) for i in range(size)])]
    ppermute x0 -> x7, waiting for transfers between devices: none -> 36.2 us  [along_ring(): return lax.ppermute(array, ('z', 'c'), pairs)]
    ppermute x30 -> x26, starting transfers between devices: 37.6 us -> 53.2 us  [shifted(): lax.ppermute(array, axis, [(i, (i + by) % size) for i in range(size)])]
    ppermute x0 -> x7, starting transfers between devices: none -> 13.4 us  [along_ring(): return lax.ppermute(array, ('z', 'c'), pairs)]
    unnamed x95 -> x79, local copies, waits for them, and re-layouts: 22.5 us -> 16.3 us
    all_to_all x1, starting transfers between devices: 10 us -> 5.89 us  [on_device(): back = lax.all_to_all(back, ('y', 'z', 'c'), 0, 0, tiled=True)]
    all_to_all x1, waiting for transfers between devices: 3.34 us -> 0.07 us  [on_device(): back = lax.all_to_all(back, ('y', 'z', 'c'), 0, 0, tiled=True)]
    pallas_call x7 -> x9, Pallas kernels: 28.3 us -> 30.7 us  [the longest x6 21.6 us: pick(): pl.pallas_call(functools.partial(pick_kernel, count), out_shape=[pltpu.HB...]
  transfers between devices with their start and end apart: 32 -> 35, of which waited for: 12 -> 13; matrix products, arithmetic and copies ran while one was open for 0% -> 1% of each run, Pallas kernels for 21% -> 22%
where the time goes in v1:
time: 277 us
  waiting for transfers between devices  106 us (38%)
  starting transfers between devices  79.9 us (29%)
  Pallas kernels  72.6 us (26%)
  local copies, waits for them, and re-layouts  17 us (6%)
    ppermute x26, waiting for transfers between devices, shifted(): lax.ppermute(array, axis, [(i, (i + by) % size) for i in range(size)])  62.3 us
    ppermute x26, starting transfers between devices, shifted(): lax.ppermute(array, axis, [(i, (i + by) % size) for i in range(size)])  53.2 us
    pallas_call x4, Pallas kernels, expert(): pl.pallas_call(functools.partial(expert_kernel, steps, chunk), grid=(step...  38.6 us
    ppermute x7, waiting for transfers between devices, along_ring(): return lax.ppermute(array, ('z', 'c'), pairs)  36.2 us
    pallas_call x6, Pallas kernels, pick(): pl.pallas_call(functools.partial(pick_kernel, count), out_shape=[pltpu.HB...  21.6 us
    unnamed x79, local copies, waits for them, and re-layouts  16.3 us
    ppermute x7, starting transfers between devices, along_ring(): return lax.ppermute(array, ('z', 'c'), pairs)  13.4 us
    all_to_all x1, starting transfers between devices, on_device(): lax.all_to_all(part.reshape(copies * NY * NC, 16, 2 * experts), ('dp', 'y...  7.46 us
  transfers between devices with their start and end apart: 35, of which 13 were waited for; matrix products, arithmetic and copies ran while one was open for 1% of the time, Pallas kernels for 22%

profile of v1, /device:TPU:1, one launch (start us, length us, event | category | flops | bytes accessed | tf_op | source)
XLA Modules:
  0.0 276.7 jit_solution(15976141646811814243)
XLA Ops:
  1.3 1.5 shard_map.230.refs_0_
  2.8 6.5 %collective-permute-start = (bf16[128,4224]{1,0:T(8,128)(2,1)S(1)}, bf16[128,4224]{1,0:T(8,128)(2,1)S(1)}, u32[]{:S(2)}, u32[]{:S(2)}) collective-permute-start(bf16[128,4224]{1,0:T(8,128)(2,1)S(1)} %shard_map.230.refs_0_), channel_id=1, source_target_pairs={{0,2},{1,15},{2,4},{3,1},{4,6},{5,3},{6,8},{7,5},{8,10},{9,7},{10,... | collective-permute-start | bytes 3244040 | tf_op jit(solution)/shard_map/ppermute | solution.py:320
  9.3 1.0 collective-permute-start.21
  10.3 21.4 %collective-permute-done.refs_0_.refs_1_ = bf16[128,4224]{1,0:T(8,128)(2,1)S(1)} collective-permute-done((bf16[128,4224]{1,0:T(8,128)(2,1)S(1)}, bf16[128,4224]{1,0:T(8,128)(2,1)S(1)}, u32[]{:S(2)}, u32[]{:S(2)}) %collective-permute-start) | collective-permute-done | bytes 1081376 | tf_op jit(solution)/shard_map/ppermute | solution.py:320
  31.7 3.4 %collective-permute-start.1 = (bf16[128,4224]{1,0:T(8,128)(2,1)S(1)}, bf16[128,4224]{1,0:T(8,128)(2,1)}, u32[]{:S(2)}, u32[]{:S(2)}) collective-permute-start(bf16[128,4224]{1,0:T(8,128)(2,1)S(1)} %collective-permute-done.refs_0_.refs_1_), channel_id=1, source_target_pairs={{0,2},{1,15},{2,4},{3,1},{4,6},{5,3},{6,8},{7,5},{8,10},{9,7},{10,... | collective-permute-start | bytes 3244040 | tf_op jit(solution)/shard_map/ppermute | solution.py:320
  35.2 3.3 %shard_map.234 = (bf16[48,4096]{1,0:T(8,128)(2,1)}, bf16[48,4096]{1,0:T(8,128)(2,1)S(1)}, bf16[48,4096]{1,0:T(8,128)(2,1)S(1)}, bf16[48,4096]{1,0:T(8,128)(2,1)S(1)}) custom-call(s32[3]{0:T(128)S(1)} %pad_add_fusion.4.here_ref, bf16[128,4224]{1,0:T(8,128)(2,1)S(1)} %shard_map.230.refs_0_, bf16[128,4224]{1,0:T(8,128)(2,1)} %collective-permute-done.21.refs_1_), custom_call_target="tpu_custom_call" | custom-call | flops 201326592 | bytes 4194304 | tf_op jit(solution)/shard_map/pallas_call | solution.py:94
  38.5 1.3 collective-permute-start.22
  39.8 2.2 collective-permute-start.25
  42.0 14.8 %collective-permute-done.1.refs_0_.refs_3_ = bf16[128,4224]{1,0:T(8,128)(2,1)} collective-permute-done((bf16[128,4224]{1,0:T(8,128)(2,1)S(1)}, bf16[128,4224]{1,0:T(8,128)(2,1)}, u32[]{:S(2)}, u32[]{:S(2)}) %collective-permute-start.1) | collective-permute-done | bytes 1081376 | tf_op jit(solution)/shard_map/ppermute | solution.py:320
  56.8 3.5 %collective-permute-start.2 = (bf16[128,4224]{1,0:T(8,128)(2,1)}, bf16[128,4224]{1,0:T(8,128)(2,1)}, u32[]{:S(2)}, u32[]{:S(2)}) collective-permute-start(bf16[128,4224]{1,0:T(8,128)(2,1)} %collective-permute-done.1.refs_0_.refs_3_), channel_id=1, source_target_pairs={{0,2},{1,15},{2,4},{3,1},{4,6},{5,3},{6,8},{7,5},{8,10},{9,7},{10,... | collective-permute-start | bytes 3244040 | tf_op jit(solution)/shard_map/ppermute | solution.py:320
  60.3 2.9 %collective-permute-start.23 = (bf16[48,4096]{1,0:T(8,128)(2,1)S(1)}, bf16[48,4096]{1,0:T(8,128)(2,1)S(1)}, u32[]{:S(2)}, u32[]{:S(2)}) collective-permute-start(bf16[48,4096]{1,0:T(8,128)(2,1)S(1)} %get-tuple-element.45), channel_id=1, source_target_pairs={{0,32},{16,48},{32,0},{48,16},{1,33},{17,49},{33,1},{49,17},{2,34}... | collective-permute-start | bytes 1179656 | tf_op jit(solution)/shard_map/ppermute | solution.py:308
  63.2 9.4 %collective-permute-done.23.refs_2_ = bf16[48,4096]{1,0:T(8,128)(2,1)S(1)} collective-permute-done((bf16[48,4096]{1,0:T(8,128)(2,1)S(1)}, bf16[48,4096]{1,0:T(8,128)(2,1)S(1)}, u32[]{:S(2)}, u32[]{:S(2)}) %collective-permute-start.23) | collective-permute-done | bytes 393248 | tf_op jit(solution)/shard_map/ppermute | solution.py:308
  72.7 2.8 %collective-permute-start.24 = (bf16[48,4096]{1,0:T(8,128)(2,1)S(1)}, bf16[48,4096]{1,0:T(8,128)(2,1)S(1)}, u32[]{:S(2)}, u32[]{:S(2)}) collective-permute-start(bf16[48,4096]{1,0:T(8,128)(2,1)S(1)} %get-tuple-element.46), channel_id=1, source_target_pairs={{0,48},{16,0},{32,16},{48,32},{1,49},{17,1},{33,17},{49,33},{2,50}... | collective-permute-start | bytes 1179656 | tf_op jit(solution)/shard_map/ppermute | solution.py:308
  75.5 7.8 %collective-permute-done.24.refs_3_ = bf16[48,4096]{1,0:T(8,128)(2,1)S(1)} collective-permute-done((bf16[48,4096]{1,0:T(8,128)(2,1)S(1)}, bf16[48,4096]{1,0:T(8,128)(2,1)S(1)}, u32[]{:S(2)}, u32[]{:S(2)}) %collective-permute-start.24) | collective-permute-done | bytes 393248 | tf_op jit(solution)/shard_map/ppermute | solution.py:308
  84.0 1.6 collective-permute-start.16
  85.6 2.6 shard_map.235
  91.6 11.6 %collective-permute-done.26.refs_5_ = bf16[48,4096]{1,0:T(8,128)(2,1)S(1)} collective-permute-done((bf16[48,4096]{1,0:T(8,128)(2,1)S(1)}, bf16[48,4096]{1,0:T(8,128)(2,1)S(1)}, u32[]{:S(2)}, u32[]{:S(2)}) %collective-permute-start.26) | collective-permute-done | bytes 393248 | tf_op jit(solution)/shard_map/ppermute | solution.py:308
  106.8 2.3 collective-permute-start.4
  109.1 1.2 copy-done.5
  110.3 2.6 shard_map.236
  112.9 4.8 %shard_map.233 = (bf16[96,4096]{1,0:T(8,128)(2,1)}, bf16[96,4096]{1,0:T(8,128)(2,1)S(1)}, bf16[96,4096]{1,0:T(8,128)(2,1)S(1)}, bf16[96,4096]{1,0:T(8,128)(2,1)S(1)}) custom-call(s32[3]{0:T(128)S(1)} %pad_add_fusion.4.here_ref, bf16[128,4224]{1,0:T(8,128)(2,1)} %collective-permute-done.1.refs_0_.refs_3_, ...), custom_call_target="tpu_custom_call" | custom-call | flops 402653184 | bytes 8388608 | tf_op jit(solution)/shard_map/pallas_call | solution.py:94
  117.7 1.3 collective-permute-start.30
  119.0 5.6 %collective-permute-done.28.refs_7_ = bf16[48,4096]{1,0:T(8,128)(2,1)S(1)} collective-permute-done((bf16[48,4096]{1,0:T(8,128)(2,1)}, bf16[48,4096]{1,0:T(8,128)(2,1)S(1)}, u32[]{:S(2)}, u32[]{:S(2)}) %collective-permute-start.28) | collective-permute-done | bytes 393248 | tf_op jit(solution)/shard_map/ppermute | solution.py:308
  125.4 2.4 collective-permute-start.32
  128.2 5.0 %shard_map.232 = (bf16[96,4096]{1,0:T(8,128)(2,1)}, bf16[96,4096]{1,0:T(8,128)(2,1)S(1)}, bf16[96,4096]{1,0:T(8,128)(2,1)S(1)}, bf16[96,4096]{1,0:T(8,128)(2,1)S(1)}) custom-call(s32[3]{0:T(128)S(1)} %pad_add_fusion.4.here_ref, bf16[128,4224]{1,0:T(8,128)(2,1)} %collective-permute-done.2.refs_0_.refs_5_, ...), custom_call_target="tpu_custom_call" | custom-call | flops 402653184 | bytes 8388608 | tf_op jit(solution)/shard_map/pallas_call | solution.py:94
  133.2 7.3 %collective-permute-start.19 = (bf16[96,4096]{1,0:T(8,128)(2,1)S(1)}, bf16[96,4096]{1,0:T(8,128)(2,1)S(1)}, u32[]{:S(2)}, u32[]{:S(2)}) collective-permute-start(bf16[96,4096]{1,0:T(8,128)(2,1)S(1)} %get-tuple-element.41), channel_id=1, source_target_pairs={{0,32},{16,48},{32,0},{48,16},{1,33},{17,49},{33,1},{49,17},{2,34}... | collective-permute-start | bytes 2359304 | tf_op jit(solution)/shard_map/ppermute | solution.py:308
  140.5 5.0 %collective-permute-done.32.refs_11_ = bf16[48,4096]{1,0:T(8,128)(2,1)S(1)} collective-permute-done((bf16[48,4096]{1,0:T(8,128)(2,1)S(1)}, bf16[48,4096]{1,0:T(8,128)(2,1)S(1)}, u32[]{:S(2)}, u32[]{:S(2)}) %collective-permute-start.32) | collective-permute-done | bytes 393248 | tf_op jit(solution)/shard_map/ppermute | solution.py:308
  145.5 1.7 collective-permute-start.13
  147.2 9.1 %collective-permute-done.18.refs_1_ = bf16[96,4096]{1,0:T(8,128)(2,1)S(1)} collective-permute-done((bf16[96,4096]{1,0:T(8,128)(2,1)S(1)}, bf16[96,4096]{1,0:T(8,128)(2,1)S(1)}, u32[]{:S(2)}, u32[]{:S(2)}) %collective-permute-start.18) | collective-permute-done | bytes 786464 | tf_op jit(solution)/shard_map/ppermute | solution.py:308
  156.3 17.8 %collective-permute-start.14 = (bf16[96,4096]{1,0:T(8,128)(2,1)S(1)}, bf16[96,4096]{1,0:T(8,128)(2,1)S(1)}, u32[]{:S(2)}, u32[]{:S(2)}) collective-permute-start(bf16[96,4096]{1,0:T(8,128)(2,1)S(1)} %get-tuple-element.37), channel_id=1, source_target_pairs={{0,32},{16,48},{32,0},{48,16},{1,33},{17,49},{33,1},{49,17},{2,34}... | collective-permute-start | bytes 2359304 | tf_op jit(solution)/shard_map/ppermute | solution.py:308
  174.3 13.8 %shard_map.237.refs_7_ = f32[8,2,128]{2,1,0:T(2,128)S(1)} custom-call(s32[2,24]{1,0:T(2,128)S(1)} %pad_add_fusion.3.table_ref, bf16[48,4096]{1,0:T(8,128)(2,1)S(1)} %copy-done.17, bf16[48,4096]{1,0:T(8,128)(2,1)S(1)} %copy-done.19, bf16[48,4096]{1,0:T(8,128)(2,1)S(1)} %copy-done.21, bf16[48,4096]{1,0:T(8,128)(2,1)S(1)} %copy-done.23, ...), custom_call_target="tpu_custom_call" | custom-call | flops 5435817984 | bytes 12582912 | tf_op jit(solution)/shard_map/pallas_call | solution.py:165
  188.1 3.3 %shard_map.231 = (bf16[48,4096]{1,0:T(8,128)(2,1)}, bf16[48,4096]{1,0:T(8,128)(2,1)S(1)}, bf16[48,4096]{1,0:T(8,128)(2,1)S(1)}, bf16[48,4096]{1,0:T(8,128)(2,1)S(1)}) custom-call(s32[3]{0:T(128)S(1)} %pad_add_fusion.4.here_ref, bf16[128,4224]{1,0:T(8,128)(2,1)} %collective-permute-done.3.refs_0_.refs_7_, bf16[128,4224]{1,0:T(8,128)(2,1)S(1)} %collective-permute-done.4.refs_1_), custom_call_target="tpu_custom_call" | custom-call | flops 201326592 | bytes 4194304 | tf_op jit(solution)/shard_map/pallas_call | solution.py:94
  191.4 1.4 collective-permute-start.5
  192.9 2.5 collective-permute-start.7
  195.4 9.9 %shard_map.238.refs_7_ = f32[8,2,128]{2,1,0:T(2,128)S(1)} custom-call(s32[2,16]{1,0:T(2,128)S(1)} %get-tuple-element.66.table_ref, bf16[96,4096]{1,0:T(8,128)(2,1)S(1)} %copy-done.15, bf16[96,4096]{1,0:T(8,128)(2,1)S(1)} %collective-permute-done.18.refs_1_, bf16[96,4096]{1,0:T(8,128)(2,1)S(1)} %collective-permute-done.19.refs_2_, ...), custom_call_target="tpu_custom_call" | custom-call | flops 3623878656 | bytes 12582912 | tf_op jit(solution)/shard_map/pallas_call | solution.py:165
  206.1 6.7 %collective-permute-done.15.refs_3_ = bf16[96,4096]{1,0:T(8,128)(2,1)S(1)} collective-permute-done((bf16[96,4096]{1,0:T(8,128)(2,1)S(1)}, bf16[96,4096]{1,0:T(8,128)(2,1)S(1)}, u32[]{:S(2)}, u32[]{:S(2)}) %collective-permute-start.15) | collective-permute-done | bytes 786464 | tf_op jit(solution)/shard_map/ppermute | solution.py:308
  212.8 10.2 %shard_map.239.refs_7_ = f32[8,2,128]{2,1,0:T(2,128)S(1)} custom-call(s32[2,16]{1,0:T(2,128)S(1)} %get-tuple-element.67.table_ref, bf16[96,4096]{1,0:T(8,128)(2,1)S(1)} %copy-done.16, bf16[96,4096]{1,0:T(8,128)(2,1)S(1)} %collective-permute-done.13.refs_1_, bf16[96,4096]{1,0:T(8,128)(2,1)S(1)} %collective-permute-done.14.refs_2_, ...), custom_call_target="tpu_custom_call" | custom-call | flops 3623878656 | bytes 12582912 | tf_op jit(solution)/shard_map/pallas_call | solution.py:165
  223.0 6.3 %collective-permute-done.7.refs_3_ = bf16[48,4096]{1,0:T(8,128)(2,1)S(1)} collective-permute-done((bf16[48,4096]{1,0:T(8,128)(2,1)S(1)}, bf16[48,4096]{1,0:T(8,128)(2,1)S(1)}, u32[]{:S(2)}, u32[]{:S(2)}) %collective-permute-start.7) | collective-permute-done | bytes 393248 | tf_op jit(solution)/shard_map/ppermute | solution.py:308
  229.4 4.7 %shard_map.240 = f32[8,2,128]{2,1,0:T(2,128)S(1)} custom-call(s32[2,8]{1,0:T(2,128)S(1)} %pad_add_fusion.2.table_ref, bf16[48,4096]{1,0:T(8,128)(2,1)S(1)} %copy-done.12, bf16[48,4096]{1,0:T(8,128)(2,1)S(1)} %collective-permute-done.5.refs_1_, bf16[48,4096]{1,0:T(8,128)(2,1)S(1)} %collective-permute-done.6.refs_2_, ...), custom_call_target="tpu_custom_call" | custom-call | flops 1811939328 | bytes 12582912 | tf_op jit(solution)/shard_map/pallas_call | solution.py:165
  234.8 5.9 %all-to-all-start = ((f32[64,2,128]{2,1,0:T(2,128)}), f32[64,2,128]{2,1,0:T(2,128)S(1)}, u32[]{:S(2)}, u32[]{:S(2)}) async-start(f32[64,2,128]{2,1,0:T(2,128)} %bitcast.15), calls=%async_computation | async-start | bytes 131072 | tf_op jit(solution)/shard_map/all_to_all | solution.py:365
  240.7 2.0 copy.25.refs_8_
  243.7 4.1 %shard_map.241 = (f32[8,128,64]{2,1,0:T(8,128)S(1)}, f32[8,128,64]{2,1,0:T(8,128)S(1)}, bf16[1024,512]{1,0:T(8,128)(2,1)S(1)}) custom-call(s32[3]{0:T(128)S(1)} %pad_add_fusion.4.here_ref, bf16[128,4224]{1,0:T(8,128)(2,1)S(1)} %shard_map.230.refs_0_, bf16[128,4224]{1,0:T(8,128)(2,1)S(1)} %collective-permute-done.refs_0_.refs_1_, ...), custom_call_target="tpu_custom_call" | custom-call | flops 1073741824 | bytes 6291456 | tf_op jit(solution)/shard_map/pallas_call | solution.py:212
  250.5 1.2 copy-done.7
  253.8 3.5 %shard_map.242 = (f32[128,64]{1,0:T(8,128)S(1)}, f32[4,8,16,128]{3,2,1,0:T(8,128)}) custom-call(s32[3]{0:T(128)S(1)} %pad_add_fusion.4.here_ref, f32[64,2,128]{2,1,0:T(2,128)S(1)} %all-to-all-done.back_ref, f32[8,128,64]{2,1,0:T(8,128)S(1)} %copy-done.9, f32[8,128,64]{2,1,0:T(8,128)S(1)} %copy-done.11, bf16[1024,512]{1,0:T(8,128)(2,1)S(1)} %copy-done.7), custom_call_target="tpu_custom_call" | custom-call | flops 268435456 | bytes 3145728 | tf_op jit(solution)/shard_map/pallas_call | solution.py:278
  257.9 7.5 %all-to-all-start.1 = ((f32[32,16,128]{2,1,0:T(8,128)}), f32[32,16,128]{2,1,0:T(8,128)S(1)}, u32[]{:S(2)}, u32[]{:S(2)}) async-start(f32[32,16,128]{2,1,0:T(8,128)} %bitcast.17), calls=%async_computation.1 | async-start | bytes 524288 | tf_op jit(solution)/shard_map/all_to_all | solution.py:373
  265.4 1.5 shard_map.243
  266.9 7.4 %all-to-all-done.1.parts_ref = f32[32,16,128]{2,1,0:T(8,128)S(1)} async-done(((f32[32,16,128]{2,1,0:T(8,128)}), f32[32,16,128]{2,1,0:T(8,128)S(1)}, u32[]{:S(2)}, u32[]{:S(2)}) %all-to-all-start.1) | async-done | bytes 262176 | tf_op jit(solution)/shard_map/all_to_all | solution.py:373
  275.0 1.7 shard_map.244
  (128 shorter events, 18.2 us)
Async XLA Ops:
  2.8 28.9 %collective-permute-start = (bf16[128,4224]{1,0:T(8,128)(2,1)S(1)}, bf16[128,4224]{1,0:T(8,128)(2,1)S(1)}, u32[]{:S(2)}, u32[]{:S(2)}) collective-permute-start(bf16[128,4224]{1,0:T(8,128)(2,1)S(1)} %shard_map.230.refs_0_), channel_id=1, source_target_pairs={{0,2},{1,15},{2,4},{3,1},{4,6},{5,3},{6,8},{7,5},{8,10},{9,7},{10,... | collective-permute-start | bytes 3244040 | tf_op jit(solution)/shard_map/ppermute | solution.py:320
  9.3 25.9 %collective-permute-start.8 = (bf16[128,4224]{1,0:T(8,128)(2,1)S(1)}, bf16[128,4224]{1,0:T(8,128)(2,1)S(1)}, u32[]{:S(2)}, u32[]{:S(2)}) collective-permute-start(bf16[128,4224]{1,0:T(8,128)(2,1)S(1)} %shard_map.230.refs_0_), channel_id=1, source_target_pairs={{0,14},{1,3},{2,0},{3,5},{4,2},{5,7},{6,4},{7,9},{8,6},{9,11},{10,... | collective-permute-start | bytes 3244040 | tf_op jit(solution)/shard_map/ppermute | solution.py:320
  9.3 25.9 %collective-permute-start.21 = (bf16[128,4224]{1,0:T(8,128)(2,1)S(1)}, bf16[128,4224]{1,0:T(8,128)(2,1)}, u32[]{:S(2)}, u32[]{:S(2)}) collective-permute-start(bf16[128,4224]{1,0:T(8,128)(2,1)S(1)} %shard_map.230.refs_0_), channel_id=1, source_target_pairs={{0,1},{1,0},{2,3},{3,2},{4,5},{5,4},{6,7},{7,6},{8,9},{9,8},{10,11... | collective-permute-start | bytes 3244040 | tf_op jit(solution)/shard_map/ppermute | solution.py:308
  31.7 25.0 %collective-permute-start.1 = (bf16[128,4224]{1,0:T(8,128)(2,1)S(1)}, bf16[128,4224]{1,0:T(8,128)(2,1)}, u32[]{:S(2)}, u32[]{:S(2)}) collective-permute-start(bf16[128,4224]{1,0:T(8,128)(2,1)S(1)} %collective-permute-done.refs_0_.refs_1_), channel_id=1, source_target_pairs={{0,2},{1,15},{2,4},{3,1},{4,6},{5,3},{6,8},{7,5},{8,10},{9,7},{10,... | collective-permute-start | bytes 3244040 | tf_op jit(solution)/shard_map/ppermute | solution.py:320
  35.2 28.0 %collective-permute-start.9 = (bf16[128,4224]{1,0:T(8,128)(2,1)S(1)}, bf16[128,4224]{1,0:T(8,128)(2,1)}, u32[]{:S(2)}, u32[]{:S(2)}) collective-permute-start(bf16[128,4224]{1,0:T(8,128)(2,1)S(1)} %collective-permute-done.8.refs_0_.refs_2_), channel_id=1, source_target_pairs={{0,14},{1,3},{2,0},{3,5},{4,2},{5,7},{6,4},{7,9},{8,6},{9,11},{10,... | collective-permute-start | bytes 3244040 | tf_op jit(solution)/shard_map/ppermute | solution.py:320
  38.5 21.7 %collective-permute-start.22 = (bf16[48,4096]{1,0:T(8,128)(2,1)S(1)}, bf16[48,4096]{1,0:T(8,128)(2,1)S(1)}, u32[]{:S(2)}, u32[]{:S(2)}) collective-permute-start(bf16[48,4096]{1,0:T(8,128)(2,1)S(1)} %get-tuple-element.44), channel_id=1, source_target_pairs={{0,16},{16,32},{32,48},{48,0},{1,17},{17,33},{33,49},{49,1},{2,18}... | collective-permute-start | bytes 1179656 | tf_op jit(solution)/shard_map/ppermute | solution.py:308
  39.8 45.8 %collective-permute-start.25 = (bf16[128,4224]{1,0:T(8,128)(2,1)S(1)}, bf16[128,4224]{1,0:T(8,128)(2,1)S(1)}, u32[]{:S(2)}, u32[]{:S(2)}) collective-permute-start(bf16[128,4224]{1,0:T(8,128)(2,1)S(1)} %collective-permute-done.refs_0_.refs_1_), channel_id=1, source_target_pairs={{0,1},{1,0},{2,3},{3,2},{4,5},{5,4},{6,7},{7,6},{8,9},{9,8},{10,11... | collective-permute-start | bytes 3244040 | tf_op jit(solution)/shard_map/ppermute | solution.py:308
  42.0 47.8 %collective-permute-start.29 = (bf16[128,4224]{1,0:T(8,128)(2,1)S(1)}, bf16[128,4224]{1,0:T(8,128)(2,1)S(1)}, u32[]{:S(2)}, u32[]{:S(2)}) collective-permute-start(bf16[128,4224]{1,0:T(8,128)(2,1)S(1)} %collective-permute-done.8.refs_0_.refs_2_), channel_id=1, source_target_pairs={{0,1},{1,0},{2,3},{3,2},{4,5},{5,4},{6,7},{7,6},{8,9},{9,8},{10,11... | collective-permute-start | bytes 3244040 | tf_op jit(solution)/shard_map/ppermute | solution.py:308
  56.8 34.9 %collective-permute-start.2 = (bf16[128,4224]{1,0:T(8,128)(2,1)}, bf16[128,4224]{1,0:T(8,128)(2,1)}, u32[]{:S(2)}, u32[]{:S(2)}) collective-permute-start(bf16[128,4224]{1,0:T(8,128)(2,1)} %collective-permute-done.1.refs_0_.refs_3_), channel_id=1, source_target_pairs={{0,2},{1,15},{2,4},{3,1},{4,6},{5,3},{6,8},{7,5},{8,10},{9,7},{10,... | collective-permute-start | bytes 3244040 | tf_op jit(solution)/shard_map/ppermute | solution.py:320
  60.3 12.3 %collective-permute-start.23 = (bf16[48,4096]{1,0:T(8,128)(2,1)S(1)}, bf16[48,4096]{1,0:T(8,128)(2,1)S(1)}, u32[]{:S(2)}, u32[]{:S(2)}) collective-permute-start(bf16[48,4096]{1,0:T(8,128)(2,1)S(1)} %get-tuple-element.45), channel_id=1, source_target_pairs={{0,32},{16,48},{32,0},{48,16},{1,33},{17,49},{33,1},{49,17},{2,34}... | collective-permute-start | bytes 1179656 | tf_op jit(solution)/shard_map/ppermute | solution.py:308
  63.2 41.8 %collective-permute-start.10 = (bf16[128,4224]{1,0:T(8,128)(2,1)}, bf16[128,4224]{1,0:T(8,128)(2,1)}, u32[]{:S(2)}, u32[]{:S(2)}) collective-permute-start(bf16[128,4224]{1,0:T(8,128)(2,1)} %collective-permute-done.9.refs_1_.refs_4_), channel_id=1, source_target_pairs={{0,14},{1,3},{2,0},{3,5},{4,2},{5,7},{6,4},{7,9},{8,6},{9,11},{10,... | collective-permute-start | bytes 3244040 | tf_op jit(solution)/shard_map/ppermute | solution.py:320
  72.6 32.4 %copy-start.38 = (s32[24]{0:T(128)S(1)}, s32[24]{0:T(128)}, u32[]{:S(2)}) copy-start(s32[24]{0:T(128)} %constant.157) | copy-start | bytes 292
  72.6 32.5 %copy-start.36 = (s32[24]{0:T(128)S(1)}, s32[24]{0:T(128)}, u32[]{:S(2)}) copy-start(s32[24]{0:T(128)} %constant.158) | copy-start | bytes 292
  72.6 34.1 %copy-start.31 = (s32[16]{0:T(128)S(1)}, s32[16]{0:T(128)}, u32[]{:S(2)}) copy-start(s32[16]{0:T(128)} %constant.143.clone) | copy-start | bytes 196
  72.6 34.1 %copy-start.35 = (s32[16]{0:T(128)S(1)}, s32[16]{0:T(128)}, u32[]{:S(2)}) copy-start(s32[16]{0:T(128)} %constant.140.clone) | copy-start | bytes 196
  72.6 36.5 %copy-start.33 = (s32[8]{0:T(128)S(1)}, s32[8]{0:T(128)}, u32[]{:S(2)}) copy-start(s32[8]{0:T(128)} %constant.145.clone) | copy-start | bytes 100
  72.6 36.4 %copy-start.34 = (s32[8]{0:T(128)S(1)}, s32[8]{0:T(128)}, u32[]{:S(2)}) copy-start(s32[8]{0:T(128)} %constant.155) | copy-start | bytes 100
  72.7 10.6 %collective-permute-start.24 = (bf16[48,4096]{1,0:T(8,128)(2,1)S(1)}, bf16[48,4096]{1,0:T(8,128)(2,1)S(1)}, u32[]{:S(2)}, u32[]{:S(2)}) collective-permute-start(bf16[48,4096]{1,0:T(8,128)(2,1)S(1)} %get-tuple-element.46), channel_id=1, source_target_pairs={{0,48},{16,0},{32,16},{48,32},{1,49},{17,1},{33,17},{49,33},{2,50}... | collective-permute-start | bytes 1179656 | tf_op jit(solution)/shard_map/ppermute | solution.py:308
  84.0 21.1 %collective-permute-start.16 = (bf16[128,4224]{1,0:T(8,128)(2,1)}, bf16[128,4224]{1,0:T(8,128)(2,1)}, u32[]{:S(2)}, u32[]{:S(2)}) collective-permute-start(bf16[128,4224]{1,0:T(8,128)(2,1)} %collective-permute-done.1.refs_0_.refs_3_), channel_id=1, source_target_pairs={{0,1},{1,0},{2,3},{3,2},{4,5},{5,4},{6,7},{7,6},{8,9},{9,8},{10,11... | collective-permute-start | bytes 3244040 | tf_op jit(solution)/shard_map/ppermute | solution.py:308
  85.6 20.1 %collective-permute-start.17 = (bf16[128,4224]{1,0:T(8,128)(2,1)}, bf16[128,4224]{1,0:T(8,128)(2,1)}, u32[]{:S(2)}, u32[]{:S(2)}) collective-permute-start(bf16[128,4224]{1,0:T(8,128)(2,1)} %collective-permute-done.9.refs_1_.refs_4_), channel_id=1, source_target_pairs={{0,1},{1,0},{2,3},{3,2},{4,5},{5,4},{6,7},{7,6},{8,9},{9,8},{10,11... | collective-permute-start | bytes 3244040 | tf_op jit(solution)/shard_map/ppermute | solution.py:308
  90.7 12.5 %collective-permute-start.26 = (bf16[48,4096]{1,0:T(8,128)(2,1)S(1)}, bf16[48,4096]{1,0:T(8,128)(2,1)S(1)}, u32[]{:S(2)}, u32[]{:S(2)}) collective-permute-start(bf16[48,4096]{1,0:T(8,128)(2,1)S(1)} %get-tuple-element.48), channel_id=1, source_target_pairs={{0,16},{16,32},{32,48},{48,0},{1,17},{17,33},{33,49},{49,1},{2,18}... | collective-permute-start | bytes 1179656 | tf_op jit(solution)/shard_map/ppermute | solution.py:308
  91.6 15.2 %collective-permute-start.3 = (bf16[128,4224]{1,0:T(8,128)(2,1)}, bf16[128,4224]{1,0:T(8,128)(2,1)}, u32[]{:S(2)}, u32[]{:S(2)}) collective-permute-start(bf16[128,4224]{1,0:T(8,128)(2,1)} %collective-permute-done.2.refs_0_.refs_5_), channel_id=1, source_target_pairs={{0,2},{1,15},{2,4},{3,1},{4,6},{5,3},{6,8},{7,5},{8,10},{9,7},{10,... | collective-permute-start | bytes 3244040 | tf_op jit(solution)/shard_map/ppermute | solution.py:320
  104.0 21.4 %collective-permute-start.11 = (bf16[128,4224]{1,0:T(8,128)(2,1)}, bf16[128,4224]{1,0:T(8,128)(2,1)}, u32[]{:S(2)}, u32[]{:S(2)}) collective-permute-start(bf16[128,4224]{1,0:T(8,128)(2,1)} %collective-permute-done.2.refs_0_.refs_5_), channel_id=1, source_target_pairs={{0,1},{1,0},{2,3},{3,2},{4,5},{5,4},{6,7},{7,6},{8,9},{9,8},{10,11... | collective-permute-start | bytes 3244040 | tf_op jit(solution)/shard_map/ppermute | solution.py:308
  105.0 22.8 %collective-permute-start.12 = (bf16[128,4224]{1,0:T(8,128)(2,1)}, bf16[128,4224]{1,0:T(8,128)(2,1)}, u32[]{:S(2)}, u32[]{:S(2)}) collective-permute-start(bf16[128,4224]{1,0:T(8,128)(2,1)} %collective-permute-done.10.refs_1_.refs_6_), channel_id=1, source_target_pairs={{0,1},{1,0},{2,3},{3,2},{4,5},{5,4},{6,7},{7,6},{8,9},{9,8},{10,11... | collective-permute-start | bytes 3244040 | tf_op jit(solution)/shard_map/ppermute | solution.py:308
  105.1 12.7 %collective-permute-start.27 = (bf16[48,4096]{1,0:T(8,128)(2,1)}, bf16[48,4096]{1,0:T(8,128)(2,1)S(1)}, u32[]{:S(2)}, u32[]{:S(2)}) collective-permute-start(bf16[48,4096]{1,0:T(8,128)(2,1)} %copy-done.29), channel_id=1, source_target_pairs={{0,32},{16,48},{32,0},{48,16},{1,33},{17,49},{33,1},{49,17},{2,34}... | collective-permute-start | bytes 1179656 | tf_op jit(solution)/shard_map/ppermute | solution.py:308
  105.7 18.9 %collective-permute-start.28 = (bf16[48,4096]{1,0:T(8,128)(2,1)}, bf16[48,4096]{1,0:T(8,128)(2,1)S(1)}, u32[]{:S(2)}, u32[]{:S(2)}) collective-permute-start(bf16[48,4096]{1,0:T(8,128)(2,1)} %copy-done.28), channel_id=1, source_target_pairs={{0,48},{16,0},{32,16},{48,32},{1,49},{17,1},{33,17},{49,33},{2,50}... | collective-permute-start | bytes 1179656 | tf_op jit(solution)/shard_map/ppermute | solution.py:308
  106.8 67.4 %collective-permute-start.4 = (bf16[128,4224]{1,0:T(8,128)(2,1)}, bf16[128,4224]{1,0:T(8,128)(2,1)S(1)}, u32[]{:S(2)}, u32[]{:S(2)}) collective-permute-start(bf16[128,4224]{1,0:T(8,128)(2,1)} %collective-permute-done.3.refs_0_.refs_7_), channel_id=1, source_target_pairs={{0,1},{1,0},{2,3},{3,2},{4,5},{5,4},{6,7},{7,6},{8,9},{9,8},{10,11... | collective-permute-start | bytes 3244040 | tf_op jit(solution)/shard_map/ppermute | solution.py:308
  117.7 15.4 %collective-permute-start.30 = (bf16[48,4096]{1,0:T(8,128)(2,1)S(1)}, bf16[48,4096]{1,0:T(8,128)(2,1)S(1)}, u32[]{:S(2)}, u32[]{:S(2)}) collective-permute-start(bf16[48,4096]{1,0:T(8,128)(2,1)S(1)} %get-tuple-element.52), channel_id=1, source_target_pairs={{0,16},{16,32},{32,48},{48,0},{1,17},{17,33},{33,49},{49,1},{2,18}... | collective-permute-start | bytes 1179656 | tf_op jit(solution)/shard_map/ppermute | solution.py:308
  124.6 15.9 %collective-permute-start.31 = (bf16[48,4096]{1,0:T(8,128)(2,1)S(1)}, bf16[48,4096]{1,0:T(8,128)(2,1)S(1)}, u32[]{:S(2)}, u32[]{:S(2)}) collective-permute-start(bf16[48,4096]{1,0:T(8,128)(2,1)S(1)} %get-tuple-element.53), channel_id=1, source_target_pairs={{0,32},{16,48},{32,0},{48,16},{1,33},{17,49},{33,1},{49,17},{2,34}... | collective-permute-start | bytes 1179656 | tf_op jit(solution)/shard_map/ppermute | solution.py:308
  125.4 20.1 %collective-permute-start.32 = (bf16[48,4096]{1,0:T(8,128)(2,1)S(1)}, bf16[48,4096]{1,0:T(8,128)(2,1)S(1)}, u32[]{:S(2)}, u32[]{:S(2)}) collective-permute-start(bf16[48,4096]{1,0:T(8,128)(2,1)S(1)} %get-tuple-element.54), channel_id=1, source_target_pairs={{0,48},{16,0},{32,16},{48,32},{1,49},{17,1},{33,17},{49,33},{2,50}... | collective-permute-start | bytes 1179656 | tf_op jit(solution)/shard_map/ppermute | solution.py:308
  127.8 28.5 %collective-permute-start.18 = (bf16[96,4096]{1,0:T(8,128)(2,1)S(1)}, bf16[96,4096]{1,0:T(8,128)(2,1)S(1)}, u32[]{:S(2)}, u32[]{:S(2)}) collective-permute-start(bf16[96,4096]{1,0:T(8,128)(2,1)S(1)} %get-tuple-element.40), channel_id=1, source_target_pairs={{0,16},{16,32},{32,48},{48,0},{1,17},{17,33},{33,49},{49,1},{2,18}... | collective-permute-start | bytes 2359304 | tf_op jit(solution)/shard_map/ppermute | solution.py:308
  128.1 46.0 %copy-start.17 = (bf16[48,4096]{1,0:T(8,128)(2,1)S(1)}, bf16[48,4096]{1,0:T(8,128)(2,1)}, u32[]{:S(2)}) copy-start(bf16[48,4096]{1,0:T(8,128)(2,1)} %get-tuple-element.43.refs_0_) | copy-start | bytes 1179652
  128.1 46.0 %copy-start.19 = (bf16[48,4096]{1,0:T(8,128)(2,1)S(1)}, bf16[48,4096]{1,0:T(8,128)(2,1)}, u32[]{:S(2)}) copy-start(bf16[48,4096]{1,0:T(8,128)(2,1)} %copy-done.18) | copy-start | bytes 1179652
  128.2 46.0 %copy-start.21 = (bf16[48,4096]{1,0:T(8,128)(2,1)S(1)}, bf16[48,4096]{1,0:T(8,128)(2,1)}, u32[]{:S(2)}) copy-start(bf16[48,4096]{1,0:T(8,128)(2,1)} %copy-done.20) | copy-start | bytes 1179652
  128.2 46.0 %copy-start.23 = (bf16[48,4096]{1,0:T(8,128)(2,1)S(1)}, bf16[48,4096]{1,0:T(8,128)(2,1)}, u32[]{:S(2)}) copy-start(bf16[48,4096]{1,0:T(8,128)(2,1)} %copy-done.22) | copy-start | bytes 1179652
  128.2 46.0 %copy-start.24 = (bf16[48,4096]{1,0:T(8,128)(2,1)S(1)}, bf16[48,4096]{1,0:T(8,128)(2,1)}, u32[]{:S(2)}) copy-start(bf16[48,4096]{1,0:T(8,128)(2,1)} %get-tuple-element.47.refs_4_) | copy-start | bytes 1179652
  128.2 46.0 %copy-start.26 = (bf16[48,4096]{1,0:T(8,128)(2,1)S(1)}, bf16[48,4096]{1,0:T(8,128)(2,1)}, u32[]{:S(2)}) copy-start(bf16[48,4096]{1,0:T(8,128)(2,1)} %copy-done.25) | copy-start | bytes 1179652
  128.2 46.0 %copy-start.27 = (bf16[48,4096]{1,0:T(8,128)(2,1)S(1)}, bf16[48,4096]{1,0:T(8,128)(2,1)}, u32[]{:S(2)}) copy-start(bf16[48,4096]{1,0:T(8,128)(2,1)} %get-tuple-element.51.refs_8_) | copy-start | bytes 1179652
  133.2 58.2 %collective-permute-start.19 = (bf16[96,4096]{1,0:T(8,128)(2,1)S(1)}, bf16[96,4096]{1,0:T(8,128)(2,1)S(1)}, u32[]{:S(2)}, u32[]{:S(2)}) collective-permute-start(bf16[96,4096]{1,0:T(8,128)(2,1)S(1)} %get-tuple-element.41), channel_id=1, source_target_pairs={{0,32},{16,48},{32,0},{48,16},{1,33},{17,49},{33,1},{49,17},{2,34}... | collective-permute-start | bytes 2359304 | tf_op jit(solution)/shard_map/ppermute | solution.py:308
  140.5 52.4 %collective-permute-start.20 = (bf16[96,4096]{1,0:T(8,128)(2,1)S(1)}, bf16[96,4096]{1,0:T(8,128)(2,1)S(1)}, u32[]{:S(2)}, u32[]{:S(2)}) collective-permute-start(bf16[96,4096]{1,0:T(8,128)(2,1)S(1)} %get-tuple-element.42), channel_id=1, source_target_pairs={{0,48},{16,0},{32,16},{48,32},{1,49},{17,1},{33,17},{49,33},{2,50}... | collective-permute-start | bytes 2359304 | tf_op jit(solution)/shard_map/ppermute | solution.py:308
  145.5 47.4 %collective-permute-start.13 = (bf16[96,4096]{1,0:T(8,128)(2,1)S(1)}, bf16[96,4096]{1,0:T(8,128)(2,1)S(1)}, u32[]{:S(2)}, u32[]{:S(2)}) collective-permute-start(bf16[96,4096]{1,0:T(8,128)(2,1)S(1)} %get-tuple-element.36), channel_id=1, source_target_pairs={{0,16},{16,32},{32,48},{48,0},{1,17},{17,33},{33,49},{49,1},{2,18}... | collective-permute-start | bytes 2359304 | tf_op jit(solution)/shard_map/ppermute | solution.py:308
  156.3 49.7 %collective-permute-start.14 = (bf16[96,4096]{1,0:T(8,128)(2,1)S(1)}, bf16[96,4096]{1,0:T(8,128)(2,1)S(1)}, u32[]{:S(2)}, u32[]{:S(2)}) collective-permute-start(bf16[96,4096]{1,0:T(8,128)(2,1)S(1)} %get-tuple-element.37), channel_id=1, source_target_pairs={{0,32},{16,48},{32,0},{48,16},{1,33},{17,49},{33,1},{49,17},{2,34}... | collective-permute-start | bytes 2359304 | tf_op jit(solution)/shard_map/ppermute | solution.py:308
  174.2 38.6 %collective-permute-start.15 = (bf16[96,4096]{1,0:T(8,128)(2,1)S(1)}, bf16[96,4096]{1,0:T(8,128)(2,1)S(1)}, u32[]{:S(2)}, u32[]{:S(2)}) collective-permute-start(bf16[96,4096]{1,0:T(8,128)(2,1)S(1)} %get-tuple-element.38), channel_id=1, source_target_pairs={{0,48},{16,0},{32,16},{48,32},{1,49},{17,1},{33,17},{49,33},{2,50}... | collective-permute-start | bytes 2359304 | tf_op jit(solution)/shard_map/ppermute | solution.py:308
  191.4 31.6 %collective-permute-start.5 = (bf16[48,4096]{1,0:T(8,128)(2,1)S(1)}, bf16[48,4096]{1,0:T(8,128)(2,1)S(1)}, u32[]{:S(2)}, u32[]{:S(2)}) collective-permute-start(bf16[48,4096]{1,0:T(8,128)(2,1)S(1)} %get-tuple-element.32), channel_id=1, source_target_pairs={{0,16},{16,32},{32,48},{48,0},{1,17},{17,33},{33,49},{49,1},{2,18}... | collective-permute-start | bytes 1179656 | tf_op jit(solution)/shard_map/ppermute | solution.py:308
  192.9 30.2 %collective-permute-start.6 = (bf16[48,4096]{1,0:T(8,128)(2,1)S(1)}, bf16[48,4096]{1,0:T(8,128)(2,1)S(1)}, u32[]{:S(2)}, u32[]{:S(2)}) collective-permute-start(bf16[48,4096]{1,0:T(8,128)(2,1)S(1)} %get-tuple-element.33), channel_id=1, source_target_pairs={{0,32},{16,48},{32,0},{48,16},{1,33},{17,49},{33,1},{49,17},{2,34}... | collective-permute-start | bytes 1179656 | tf_op jit(solution)/shard_map/ppermute | solution.py:308
  192.9 36.5 %collective-permute-start.7 = (bf16[48,4096]{1,0:T(8,128)(2,1)S(1)}, bf16[48,4096]{1,0:T(8,128)(2,1)S(1)}, u32[]{:S(2)}, u32[]{:S(2)}) collective-permute-start(bf16[48,4096]{1,0:T(8,128)(2,1)S(1)} %get-tuple-element.34), channel_id=1, source_target_pairs={{0,48},{16,0},{32,16},{48,32},{1,49},{17,1},{33,17},{49,33},{2,50}... | collective-permute-start | bytes 1179656 | tf_op jit(solution)/shard_map/ppermute | solution.py:308
  234.8 15.7 %all-to-all-start = ((f32[64,2,128]{2,1,0:T(2,128)}), f32[64,2,128]{2,1,0:T(2,128)S(1)}, u32[]{:S(2)}, u32[]{:S(2)}) async-start(f32[64,2,128]{2,1,0:T(2,128)} %bitcast.15), calls=%async_computation | async-start | bytes 131072 | tf_op jit(solution)/shard_map/all_to_all | solution.py:365
  257.9 16.4 %all-to-all-start.1 = ((f32[32,16,128]{2,1,0:T(8,128)}), f32[32,16,128]{2,1,0:T(8,128)S(1)}, u32[]{:S(2)}, u32[]{:S(2)}) async-start(f32[32,16,128]{2,1,0:T(8,128)} %bitcast.17), calls=%async_computation.1 | async-start | bytes 524288 | tf_op jit(solution)/shard_map/all_to_all | solution.py:373
  (26 other events, 196.5 us)

commit v2 on v1

--- a/solution.py
+++ b/solution.py
@@ -278,7 +278,7 @@
     return pl.pallas_call(
         finish_kernel,
         out_shape=[
-            jax.ShapeDtypeStruct((rows, experts), jnp.float32),
+            pltpu.HBM((rows, experts), jnp.float32),
             jax.ShapeDtypeStruct((copies, NY * NC, 16, 2 * experts), jnp.float32),
         ],
         in_specs=in_smem() + in_vmem(4),
@@ -343,7 +343,9 @@
         slices = [ring[key] for key in group]
         slices = slices + [shifted(a, "c", 1) for a in slices]
         rows = pick(here, slices)
-        arrived.append([rows[0]] + [shifted(rows[dy], "y", dy) for dy in range(1, NY)])
+        near = [shifted(rows[dy], "y", dy) for dy in (1, 3)]
+        far = shifted(rows[2], "y", 2)
+        arrived.append([rows[0], near[0], far, near[1]])
 
     products = jnp.zeros((NY * NC, NZ // PACK, 128), jnp.float32)
     for i, members in enumerate(((0, 1, 2), (3,), (4,), (5,))):
@@ -375,7 +377,7 @@
     )
     router_grad = pl.pallas_call(
         sum_kernel, out_shape=jax.ShapeDtypeStruct((32, experts), jnp.float32)
-    )(parts)
+    )(in_hbm(parts))
     return (gate_grad, router_grad)
 
 

time: 277 us -> 277 us (level)
    unnamed x79 -> x77, local copies, waits for them, and re-layouts: 16.3 us -> 15.6 us
where the time goes in v2:
time: 277 us; the launch traced here: 276 us
  waiting for transfers between devices  106 us (38%)
  starting transfers between devices  79.8 us (29%)
  Pallas kernels  72.5 us (26%)
  local copies, waits for them, and re-layouts  16.3 us (6%)
    ppermute x26, waiting for transfers between devices, shifted(): lax.ppermute(array, axis, [(i, (i + by) % size) for i in range(size)])  62.4 us
    ppermute x26, starting transfers between devices, shifted(): lax.ppermute(array, axis, [(i, (i + by) % size) for i in range(size)])  53.1 us
    pallas_call x4, Pallas kernels, expert(): pl.pallas_call(functools.partial(expert_kernel, steps, chunk), grid=(step...  38.7 us
    ppermute x7, waiting for transfers between devices, along_ring(): return lax.ppermute(array, ('z', 'c'), pairs)  36.2 us
    pallas_call x6, Pallas kernels, pick(): pl.pallas_call(functools.partial(pick_kernel, count), out_shape=[pltpu.HB...  21.6 us
    unnamed x77, local copies, waits for them, and re-layouts  15.6 us
    ppermute x7, starting transfers between devices, along_ring(): return lax.ppermute(array, ('z', 'c'), pairs)  13.4 us
    all_to_all x1, starting transfers between devices, on_device(): lax.all_to_all(part.reshape(copies * NY * NC, 16, 2 * experts), ('dp', 'y...  7.43 us
  transfers between devices with their start and end apart: 35, of which 13 were waited for; matrix products, arithmetic and copies ran while one was open for 1% of the time, Pallas kernels for 22%

profile of v2, /device:TPU:1, one launch (start us, length us, event | category | flops | bytes accessed | tf_op | source)
XLA Modules:
  0.0 275.9 jit_solution(3707724473713140833)
XLA Ops:
  1.3 1.5 shard_map.230.refs_0_
  2.8 6.5 %collective-permute-start = (bf16[128,4224]{1,0:T(8,128)(2,1)S(1)}, bf16[128,4224]{1,0:T(8,128)(2,1)S(1)}, u32[]{:S(2)}, u32[]{:S(2)}) collective-permute-start(bf16[128,4224]{1,0:T(8,128)(2,1)S(1)} %shard_map.230.refs_0_), channel_id=1, source_target_pairs={{0,2},{1,15},{2,4},{3,1},{4,6},{5,3},{6,8},{7,5},{8,10},{9,7},{10,... | collective-permute-start | bytes 3244040 | tf_op jit(solution)/shard_map/ppermute | solution.py:320
  9.3 1.0 collective-permute-start.21
  10.3 21.4 %collective-permute-done.refs_0_.refs_1_ = bf16[128,4224]{1,0:T(8,128)(2,1)S(1)} collective-permute-done((bf16[128,4224]{1,0:T(8,128)(2,1)S(1)}, bf16[128,4224]{1,0:T(8,128)(2,1)S(1)}, u32[]{:S(2)}, u32[]{:S(2)}) %collective-permute-start) | collective-permute-done | bytes 1081376 | tf_op jit(solution)/shard_map/ppermute | solution.py:320
  31.7 3.4 %collective-permute-start.1 = (bf16[128,4224]{1,0:T(8,128)(2,1)S(1)}, bf16[128,4224]{1,0:T(8,128)(2,1)}, u32[]{:S(2)}, u32[]{:S(2)}) collective-permute-start(bf16[128,4224]{1,0:T(8,128)(2,1)S(1)} %collective-permute-done.refs_0_.refs_1_), channel_id=1, source_target_pairs={{0,2},{1,15},{2,4},{3,1},{4,6},{5,3},{6,8},{7,5},{8,10},{9,7},{10,... | collective-permute-start | bytes 3244040 | tf_op jit(solution)/shard_map/ppermute | solution.py:320
  35.2 3.3 %shard_map.234 = (bf16[48,4096]{1,0:T(8,128)(2,1)}, bf16[48,4096]{1,0:T(8,128)(2,1)S(1)}, bf16[48,4096]{1,0:T(8,128)(2,1)S(1)}, bf16[48,4096]{1,0:T(8,128)(2,1)S(1)}) custom-call(s32[3]{0:T(128)S(1)} %pad_add_fusion.4.here_ref, bf16[128,4224]{1,0:T(8,128)(2,1)S(1)} %shard_map.230.refs_0_, bf16[128,4224]{1,0:T(8,128)(2,1)} %collective-permute-done.21.refs_1_), custom_call_target="tpu_custom_call" | custom-call | flops 201326592 | bytes 4194304 | tf_op jit(solution)/shard_map/pallas_call | solution.py:94
  38.5 1.3 collective-permute-start.22
  39.8 2.2 collective-permute-start.25
  42.0 14.7 %collective-permute-done.1.refs_0_.refs_3_ = bf16[128,4224]{1,0:T(8,128)(2,1)} collective-permute-done((bf16[128,4224]{1,0:T(8,128)(2,1)S(1)}, bf16[128,4224]{1,0:T(8,128)(2,1)}, u32[]{:S(2)}, u32[]{:S(2)}) %collective-permute-start.1) | collective-permute-done | bytes 1081376 | tf_op jit(solution)/shard_map/ppermute | solution.py:320
  56.8 3.5 %collective-permute-start.2 = (bf16[128,4224]{1,0:T(8,128)(2,1)}, bf16[128,4224]{1,0:T(8,128)(2,1)}, u32[]{:S(2)}, u32[]{:S(2)}) collective-permute-start(bf16[128,4224]{1,0:T(8,128)(2,1)} %collective-permute-done.1.refs_0_.refs_3_), channel_id=1, source_target_pairs={{0,2},{1,15},{2,4},{3,1},{4,6},{5,3},{6,8},{7,5},{8,10},{9,7},{10,... | collective-permute-start | bytes 3244040 | tf_op jit(solution)/shard_map/ppermute | solution.py:320
  60.3 2.9 %collective-permute-start.23 = (bf16[48,4096]{1,0:T(8,128)(2,1)S(1)}, bf16[48,4096]{1,0:T(8,128)(2,1)S(1)}, u32[]{:S(2)}, u32[]{:S(2)}) collective-permute-start(bf16[48,4096]{1,0:T(8,128)(2,1)S(1)} %get-tuple-element.45), channel_id=1, source_target_pairs={{0,32},{16,48},{32,0},{48,16},{1,33},{17,49},{33,1},{49,17},{2,34}... | collective-permute-start | bytes 1179656 | tf_op jit(solution)/shard_map/ppermute | solution.py:308
  63.2 9.4 %collective-permute-done.23.refs_2_ = bf16[48,4096]{1,0:T(8,128)(2,1)S(1)} collective-permute-done((bf16[48,4096]{1,0:T(8,128)(2,1)S(1)}, bf16[48,4096]{1,0:T(8,128)(2,1)S(1)}, u32[]{:S(2)}, u32[]{:S(2)}) %collective-permute-start.23) | collective-permute-done | bytes 393248 | tf_op jit(solution)/shard_map/ppermute | solution.py:308
  72.7 2.8 %collective-permute-start.24 = (bf16[48,4096]{1,0:T(8,128)(2,1)S(1)}, bf16[48,4096]{1,0:T(8,128)(2,1)S(1)}, u32[]{:S(2)}, u32[]{:S(2)}) collective-permute-start(bf16[48,4096]{1,0:T(8,128)(2,1)S(1)} %get-tuple-element.46), channel_id=1, source_target_pairs={{0,48},{16,0},{32,16},{48,32},{1,49},{17,1},{33,17},{49,33},{2,50}... | collective-permute-start | bytes 1179656 | tf_op jit(solution)/shard_map/ppermute | solution.py:308
  75.5 7.8 %collective-permute-done.24.refs_3_ = bf16[48,4096]{1,0:T(8,128)(2,1)S(1)} collective-permute-done((bf16[48,4096]{1,0:T(8,128)(2,1)S(1)}, bf16[48,4096]{1,0:T(8,128)(2,1)S(1)}, u32[]{:S(2)}, u32[]{:S(2)}) %collective-permute-start.24) | collective-permute-done | bytes 393248 | tf_op jit(solution)/shard_map/ppermute | solution.py:308
  84.0 1.6 collective-permute-start.16
  85.6 2.6 shard_map.235
  91.6 11.6 %collective-permute-done.26.refs_5_ = bf16[48,4096]{1,0:T(8,128)(2,1)S(1)} collective-permute-done((bf16[48,4096]{1,0:T(8,128)(2,1)S(1)}, bf16[48,4096]{1,0:T(8,128)(2,1)S(1)}, u32[]{:S(2)}, u32[]{:S(2)}) %collective-permute-start.26) | collective-permute-done | bytes 393248 | tf_op jit(solution)/shard_map/ppermute | solution.py:308
  106.7 2.3 collective-permute-start.4
  109.1 1.2 copy-done.5
  110.3 2.6 shard_map.236
  112.9 4.8 %shard_map.233 = (bf16[96,4096]{1,0:T(8,128)(2,1)}, bf16[96,4096]{1,0:T(8,128)(2,1)S(1)}, bf16[96,4096]{1,0:T(8,128)(2,1)S(1)}, bf16[96,4096]{1,0:T(8,128)(2,1)S(1)}) custom-call(s32[3]{0:T(128)S(1)} %pad_add_fusion.4.here_ref, bf16[128,4224]{1,0:T(8,128)(2,1)} %collective-permute-done.1.refs_0_.refs_3_, ...), custom_call_target="tpu_custom_call" | custom-call | flops 402653184 | bytes 8388608 | tf_op jit(solution)/shard_map/pallas_call | solution.py:94
  117.7 1.3 collective-permute-start.30
  119.0 5.6 %collective-permute-done.28.refs_7_ = bf16[48,4096]{1,0:T(8,128)(2,1)S(1)} collective-permute-done((bf16[48,4096]{1,0:T(8,128)(2,1)}, bf16[48,4096]{1,0:T(8,128)(2,1)S(1)}, u32[]{:S(2)}, u32[]{:S(2)}) %collective-permute-start.28) | collective-permute-done | bytes 393248 | tf_op jit(solution)/shard_map/ppermute | solution.py:308
  125.4 2.4 collective-permute-start.32
  128.2 5.0 %shard_map.232 = (bf16[96,4096]{1,0:T(8,128)(2,1)}, bf16[96,4096]{1,0:T(8,128)(2,1)S(1)}, bf16[96,4096]{1,0:T(8,128)(2,1)S(1)}, bf16[96,4096]{1,0:T(8,128)(2,1)S(1)}) custom-call(s32[3]{0:T(128)S(1)} %pad_add_fusion.4.here_ref, bf16[128,4224]{1,0:T(8,128)(2,1)} %collective-permute-done.2.refs_0_.refs_5_, ...), custom_call_target="tpu_custom_call" | custom-call | flops 402653184 | bytes 8388608 | tf_op jit(solution)/shard_map/pallas_call | solution.py:94
  133.2 7.3 %collective-permute-start.19 = (bf16[96,4096]{1,0:T(8,128)(2,1)S(1)}, bf16[96,4096]{1,0:T(8,128)(2,1)S(1)}, u32[]{:S(2)}, u32[]{:S(2)}) collective-permute-start(bf16[96,4096]{1,0:T(8,128)(2,1)S(1)} %get-tuple-element.41), channel_id=1, source_target_pairs={{0,32},{16,48},{32,0},{48,16},{1,33},{17,49},{33,1},{49,17},{2,34}... | collective-permute-start | bytes 2359304 | tf_op jit(solution)/shard_map/ppermute | solution.py:308
  140.4 5.0 %collective-permute-done.32.refs_11_ = bf16[48,4096]{1,0:T(8,128)(2,1)S(1)} collective-permute-done((bf16[48,4096]{1,0:T(8,128)(2,1)S(1)}, bf16[48,4096]{1,0:T(8,128)(2,1)S(1)}, u32[]{:S(2)}, u32[]{:S(2)}) %collective-permute-start.32) | collective-permute-done | bytes 393248 | tf_op jit(solution)/shard_map/ppermute | solution.py:308
  145.5 1.7 collective-permute-start.13
  147.2 9.1 %collective-permute-done.18.refs_1_ = bf16[96,4096]{1,0:T(8,128)(2,1)S(1)} collective-permute-done((bf16[96,4096]{1,0:T(8,128)(2,1)S(1)}, bf16[96,4096]{1,0:T(8,128)(2,1)S(1)}, u32[]{:S(2)}, u32[]{:S(2)}) %collective-permute-start.18) | collective-permute-done | bytes 786464 | tf_op jit(solution)/shard_map/ppermute | solution.py:308
  156.3 17.8 %collective-permute-start.14 = (bf16[96,4096]{1,0:T(8,128)(2,1)S(1)}, bf16[96,4096]{1,0:T(8,128)(2,1)S(1)}, u32[]{:S(2)}, u32[]{:S(2)}) collective-permute-start(bf16[96,4096]{1,0:T(8,128)(2,1)S(1)} %get-tuple-element.37), channel_id=1, source_target_pairs={{0,32},{16,48},{32,0},{48,16},{1,33},{17,49},{33,1},{49,17},{2,34}... | collective-permute-start | bytes 2359304 | tf_op jit(solution)/shard_map/ppermute | solution.py:308
  174.2 13.8 %shard_map.237.refs_7_ = f32[8,2,128]{2,1,0:T(2,128)S(1)} custom-call(s32[2,24]{1,0:T(2,128)S(1)} %pad_add_fusion.3.table_ref, bf16[48,4096]{1,0:T(8,128)(2,1)S(1)} %copy-done.16, bf16[48,4096]{1,0:T(8,128)(2,1)S(1)} %copy-done.18, bf16[48,4096]{1,0:T(8,128)(2,1)S(1)} %copy-done.20, bf16[48,4096]{1,0:T(8,128)(2,1)S(1)} %copy-done.22, ...), custom_call_target="tpu_custom_call" | custom-call | flops 5435817984 | bytes 12582912 | tf_op jit(solution)/shard_map/pallas_call | solution.py:165
  188.0 3.3 %shard_map.231 = (bf16[48,4096]{1,0:T(8,128)(2,1)}, bf16[48,4096]{1,0:T(8,128)(2,1)S(1)}, bf16[48,4096]{1,0:T(8,128)(2,1)S(1)}, bf16[48,4096]{1,0:T(8,128)(2,1)S(1)}) custom-call(s32[3]{0:T(128)S(1)} %pad_add_fusion.4.here_ref, bf16[128,4224]{1,0:T(8,128)(2,1)} %collective-permute-done.3.refs_0_.refs_7_, bf16[128,4224]{1,0:T(8,128)(2,1)S(1)} %collective-permute-done.4.refs_1_), custom_call_target="tpu_custom_call" | custom-call | flops 201326592 | bytes 4194304 | tf_op jit(solution)/shard_map/pallas_call | solution.py:94
  191.3 1.4 collective-permute-start.5
  192.8 2.5 collective-permute-start.7
  195.3 9.9 %shard_map.238.refs_7_ = f32[8,2,128]{2,1,0:T(2,128)S(1)} custom-call(s32[2,16]{1,0:T(2,128)S(1)} %get-tuple-element.66.table_ref, bf16[96,4096]{1,0:T(8,128)(2,1)S(1)} %copy-done.14, bf16[96,4096]{1,0:T(8,128)(2,1)S(1)} %collective-permute-done.18.refs_1_, bf16[96,4096]{1,0:T(8,128)(2,1)S(1)} %collective-permute-done.19.refs_2_, ...), custom_call_target="tpu_custom_call" | custom-call | flops 3623878656 | bytes 12582912 | tf_op jit(solution)/shard_map/pallas_call | solution.py:165
  206.0 6.8 %collective-permute-done.15.refs_3_ = bf16[96,4096]{1,0:T(8,128)(2,1)S(1)} collective-permute-done((bf16[96,4096]{1,0:T(8,128)(2,1)S(1)}, bf16[96,4096]{1,0:T(8,128)(2,1)S(1)}, u32[]{:S(2)}, u32[]{:S(2)}) %collective-permute-start.15) | collective-permute-done | bytes 786464 | tf_op jit(solution)/shard_map/ppermute | solution.py:308
  212.8 10.2 %shard_map.239.refs_7_ = f32[8,2,128]{2,1,0:T(2,128)S(1)} custom-call(s32[2,16]{1,0:T(2,128)S(1)} %get-tuple-element.67.table_ref, bf16[96,4096]{1,0:T(8,128)(2,1)S(1)} %copy-done.15, bf16[96,4096]{1,0:T(8,128)(2,1)S(1)} %collective-permute-done.13.refs_1_, bf16[96,4096]{1,0:T(8,128)(2,1)S(1)} %collective-permute-done.14.refs_2_, ...), custom_call_target="tpu_custom_call" | custom-call | flops 3623878656 | bytes 12582912 | tf_op jit(solution)/shard_map/pallas_call | solution.py:165
  223.0 6.3 %collective-permute-done.7.refs_3_ = bf16[48,4096]{1,0:T(8,128)(2,1)S(1)} collective-permute-done((bf16[48,4096]{1,0:T(8,128)(2,1)S(1)}, bf16[48,4096]{1,0:T(8,128)(2,1)S(1)}, u32[]{:S(2)}, u32[]{:S(2)}) %collective-permute-start.7) | collective-permute-done | bytes 393248 | tf_op jit(solution)/shard_map/ppermute | solution.py:308
  229.4 4.7 %shard_map.240 = f32[8,2,128]{2,1,0:T(2,128)S(1)} custom-call(s32[2,8]{1,0:T(2,128)S(1)} %pad_add_fusion.2.table_ref, bf16[48,4096]{1,0:T(8,128)(2,1)S(1)} %copy-done.12, bf16[48,4096]{1,0:T(8,128)(2,1)S(1)} %collective-permute-done.5.refs_1_, bf16[48,4096]{1,0:T(8,128)(2,1)S(1)} %collective-permute-done.6.refs_2_, ...), custom_call_target="tpu_custom_call" | custom-call | flops 1811939328 | bytes 12582912 | tf_op jit(solution)/shard_map/pallas_call | solution.py:165
  234.8 5.9 %all-to-all-start = ((f32[64,2,128]{2,1,0:T(2,128)}), f32[64,2,128]{2,1,0:T(2,128)S(1)}, u32[]{:S(2)}, u32[]{:S(2)}) async-start(f32[64,2,128]{2,1,0:T(2,128)} %bitcast.15), calls=%async_computation | async-start | bytes 131072 | tf_op jit(solution)/shard_map/all_to_all | solution.py:367
  240.6 2.0 copy.25.refs_8_
  243.7 4.1 %shard_map.241 = (f32[8,128,64]{2,1,0:T(8,128)S(1)}, f32[8,128,64]{2,1,0:T(8,128)S(1)}, bf16[1024,512]{1,0:T(8,128)(2,1)S(1)}) custom-call(s32[3]{0:T(128)S(1)} %pad_add_fusion.4.here_ref, bf16[128,4224]{1,0:T(8,128)(2,1)S(1)} %shard_map.230.refs_0_, bf16[128,4224]{1,0:T(8,128)(2,1)S(1)} %collective-permute-done.refs_0_.refs_1_, ...), custom_call_target="tpu_custom_call" | custom-call | flops 1073741824 | bytes 6291456 | tf_op jit(solution)/shard_map/pallas_call | solution.py:212
  250.4 1.2 copy-done.7
  253.7 3.5 %shard_map.242 = (f32[128,64]{1,0:T(8,128)}, f32[4,8,16,128]{3,2,1,0:T(8,128)}) custom-call(s32[3]{0:T(128)S(1)} %pad_add_fusion.4.here_ref, f32[64,2,128]{2,1,0:T(2,128)S(1)} %all-to-all-done.back_ref, f32[8,128,64]{2,1,0:T(8,128)S(1)} %copy-done.9, f32[8,128,64]{2,1,0:T(8,128)S(1)} %copy-done.11, bf16[1024,512]{1,0:T(8,128)(2,1)S(1)} %copy-done.7), custom_call_target="tpu_custom_call" | custom-call | flops 268435456 | bytes 3145728 | tf_op jit(solution)/shard_map/pallas_call | solution.py:278
  257.2 7.4 %all-to-all-start.1 = ((f32[32,16,128]{2,1,0:T(8,128)}), f32[32,16,128]{2,1,0:T(8,128)S(1)}, u32[]{:S(2)}, u32[]{:S(2)}) async-start(f32[32,16,128]{2,1,0:T(8,128)} %bitcast.17), calls=%async_computation.1 | async-start | bytes 524288 | tf_op jit(solution)/shard_map/all_to_all | solution.py:375
  264.6 1.5 shard_map.243
  266.2 7.4 %all-to-all-done.1.parts_ref = f32[32,16,128]{2,1,0:T(8,128)S(1)} async-done(((f32[32,16,128]{2,1,0:T(8,128)}), f32[32,16,128]{2,1,0:T(8,128)S(1)}, u32[]{:S(2)}, u32[]{:S(2)}) %all-to-all-start.1) | async-done | bytes 262176 | tf_op jit(solution)/shard_map/all_to_all | solution.py:375
  274.3 1.7 shard_map.244
  (126 shorter events, 17.5 us)
Async XLA Ops:
  2.8 28.9 %collective-permute-start = (bf16[128,4224]{1,0:T(8,128)(2,1)S(1)}, bf16[128,4224]{1,0:T(8,128)(2,1)S(1)}, u32[]{:S(2)}, u32[]{:S(2)}) collective-permute-start(bf16[128,4224]{1,0:T(8,128)(2,1)S(1)} %shard_map.230.refs_0_), channel_id=1, source_target_pairs={{0,2},{1,15},{2,4},{3,1},{4,6},{5,3},{6,8},{7,5},{8,10},{9,7},{10,... | collective-permute-start | bytes 3244040 | tf_op jit(solution)/shard_map/ppermute | solution.py:320
  9.3 25.9 %collective-permute-start.8 = (bf16[128,4224]{1,0:T(8,128)(2,1)S(1)}, bf16[128,4224]{1,0:T(8,128)(2,1)S(1)}, u32[]{:S(2)}, u32[]{:S(2)}) collective-permute-start(bf16[128,4224]{1,0:T(8,128)(2,1)S(1)} %shard_map.230.refs_0_), channel_id=1, source_target_pairs={{0,14},{1,3},{2,0},{3,5},{4,2},{5,7},{6,4},{7,9},{8,6},{9,11},{10,... | collective-permute-start | bytes 3244040 | tf_op jit(solution)/shard_map/ppermute | solution.py:320
  9.3 25.9 %collective-permute-start.21 = (bf16[128,4224]{1,0:T(8,128)(2,1)S(1)}, bf16[128,4224]{1,0:T(8,128)(2,1)}, u32[]{:S(2)}, u32[]{:S(2)}) collective-permute-start(bf16[128,4224]{1,0:T(8,128)(2,1)S(1)} %shard_map.230.refs_0_), channel_id=1, source_target_pairs={{0,1},{1,0},{2,3},{3,2},{4,5},{5,4},{6,7},{7,6},{8,9},{9,8},{10,11... | collective-permute-start | bytes 3244040 | tf_op jit(solution)/shard_map/ppermute | solution.py:308
  31.7 25.0 %collective-permute-start.1 = (bf16[128,4224]{1,0:T(8,128)(2,1)S(1)}, bf16[128,4224]{1,0:T(8,128)(2,1)}, u32[]{:S(2)}, u32[]{:S(2)}) collective-permute-start(bf16[128,4224]{1,0:T(8,128)(2,1)S(1)} %collective-permute-done.refs_0_.refs_1_), channel_id=1, source_target_pairs={{0,2},{1,15},{2,4},{3,1},{4,6},{5,3},{6,8},{7,5},{8,10},{9,7},{10,... | collective-permute-start | bytes 3244040 | tf_op jit(solution)/shard_map/ppermute | solution.py:320
  35.2 28.0 %collective-permute-start.9 = (bf16[128,4224]{1,0:T(8,128)(2,1)S(1)}, bf16[128,4224]{1,0:T(8,128)(2,1)}, u32[]{:S(2)}, u32[]{:S(2)}) collective-permute-start(bf16[128,4224]{1,0:T(8,128)(2,1)S(1)} %collective-permute-done.8.refs_0_.refs_2_), channel_id=1, source_target_pairs={{0,14},{1,3},{2,0},{3,5},{4,2},{5,7},{6,4},{7,9},{8,6},{9,11},{10,... | collective-permute-start | bytes 3244040 | tf_op jit(solution)/shard_map/ppermute | solution.py:320
  38.5 21.7 %collective-permute-start.22 = (bf16[48,4096]{1,0:T(8,128)(2,1)S(1)}, bf16[48,4096]{1,0:T(8,128)(2,1)S(1)}, u32[]{:S(2)}, u32[]{:S(2)}) collective-permute-start(bf16[48,4096]{1,0:T(8,128)(2,1)S(1)} %get-tuple-element.44), channel_id=1, source_target_pairs={{0,16},{16,32},{32,48},{48,0},{1,17},{17,33},{33,49},{49,1},{2,18}... | collective-permute-start | bytes 1179656 | tf_op jit(solution)/shard_map/ppermute | solution.py:308
  39.8 45.8 %collective-permute-start.25 = (bf16[128,4224]{1,0:T(8,128)(2,1)S(1)}, bf16[128,4224]{1,0:T(8,128)(2,1)S(1)}, u32[]{:S(2)}, u32[]{:S(2)}) collective-permute-start(bf16[128,4224]{1,0:T(8,128)(2,1)S(1)} %collective-permute-done.refs_0_.refs_1_), channel_id=1, source_target_pairs={{0,1},{1,0},{2,3},{3,2},{4,5},{5,4},{6,7},{7,6},{8,9},{9,8},{10,11... | collective-permute-start | bytes 3244040 | tf_op jit(solution)/shard_map/ppermute | solution.py:308
  42.0 47.7 %collective-permute-start.29 = (bf16[128,4224]{1,0:T(8,128)(2,1)S(1)}, bf16[128,4224]{1,0:T(8,128)(2,1)S(1)}, u32[]{:S(2)}, u32[]{:S(2)}) collective-permute-start(bf16[128,4224]{1,0:T(8,128)(2,1)S(1)} %collective-permute-done.8.refs_0_.refs_2_), channel_id=1, source_target_pairs={{0,1},{1,0},{2,3},{3,2},{4,5},{5,4},{6,7},{7,6},{8,9},{9,8},{10,11... | collective-permute-start | bytes 3244040 | tf_op jit(solution)/shard_map/ppermute | solution.py:308
  56.8 34.8 %collective-permute-start.2 = (bf16[128,4224]{1,0:T(8,128)(2,1)}, bf16[128,4224]{1,0:T(8,128)(2,1)}, u32[]{:S(2)}, u32[]{:S(2)}) collective-permute-start(bf16[128,4224]{1,0:T(8,128)(2,1)} %collective-permute-done.1.refs_0_.refs_3_), channel_id=1, source_target_pairs={{0,2},{1,15},{2,4},{3,1},{4,6},{5,3},{6,8},{7,5},{8,10},{9,7},{10,... | collective-permute-start | bytes 3244040 | tf_op jit(solution)/shard_map/ppermute | solution.py:320
  60.3 12.3 %collective-permute-start.23 = (bf16[48,4096]{1,0:T(8,128)(2,1)S(1)}, bf16[48,4096]{1,0:T(8,128)(2,1)S(1)}, u32[]{:S(2)}, u32[]{:S(2)}) collective-permute-start(bf16[48,4096]{1,0:T(8,128)(2,1)S(1)} %get-tuple-element.45), channel_id=1, source_target_pairs={{0,32},{16,48},{32,0},{48,16},{1,33},{17,49},{33,1},{49,17},{2,34}... | collective-permute-start | bytes 1179656 | tf_op jit(solution)/shard_map/ppermute | solution.py:308
  63.2 41.8 %collective-permute-start.10 = (bf16[128,4224]{1,0:T(8,128)(2,1)}, bf16[128,4224]{1,0:T(8,128)(2,1)}, u32[]{:S(2)}, u32[]{:S(2)}) collective-permute-start(bf16[128,4224]{1,0:T(8,128)(2,1)} %collective-permute-done.9.refs_1_.refs_4_), channel_id=1, source_target_pairs={{0,14},{1,3},{2,0},{3,5},{4,2},{5,7},{6,4},{7,9},{8,6},{9,11},{10,... | collective-permute-start | bytes 3244040 | tf_op jit(solution)/shard_map/ppermute | solution.py:320
  72.6 32.4 %copy-start.37 = (s32[24]{0:T(128)S(1)}, s32[24]{0:T(128)}, u32[]{:S(2)}) copy-start(s32[24]{0:T(128)} %constant.157) | copy-start | bytes 292
  72.6 32.4 %copy-start.35 = (s32[24]{0:T(128)S(1)}, s32[24]{0:T(128)}, u32[]{:S(2)}) copy-start(s32[24]{0:T(128)} %constant.158) | copy-start | bytes 292
  72.6 34.1 %copy-start.30 = (s32[16]{0:T(128)S(1)}, s32[16]{0:T(128)}, u32[]{:S(2)}) copy-start(s32[16]{0:T(128)} %constant.143.clone) | copy-start | bytes 196
  72.6 34.1 %copy-start.34 = (s32[16]{0:T(128)S(1)}, s32[16]{0:T(128)}, u32[]{:S(2)}) copy-start(s32[16]{0:T(128)} %constant.140.clone) | copy-start | bytes 196
  72.6 36.4 %copy-start.32 = (s32[8]{0:T(128)S(1)}, s32[8]{0:T(128)}, u32[]{:S(2)}) copy-start(s32[8]{0:T(128)} %constant.145.clone) | copy-start | bytes 100
  72.6 36.4 %copy-start.33 = (s32[8]{0:T(128)S(1)}, s32[8]{0:T(128)}, u32[]{:S(2)}) copy-start(s32[8]{0:T(128)} %constant.155) | copy-start | bytes 100
  72.7 10.6 %collective-permute-start.24 = (bf16[48,4096]{1,0:T(8,128)(2,1)S(1)}, bf16[48,4096]{1,0:T(8,128)(2,1)S(1)}, u32[]{:S(2)}, u32[]{:S(2)}) collective-permute-start(bf16[48,4096]{1,0:T(8,128)(2,1)S(1)} %get-tuple-element.46), channel_id=1, source_target_pairs={{0,48},{16,0},{32,16},{48,32},{1,49},{17,1},{33,17},{49,33},{2,50}... | collective-permute-start | bytes 1179656 | tf_op jit(solution)/shard_map/ppermute | solution.py:308
  84.0 21.1 %collective-permute-start.16 = (bf16[128,4224]{1,0:T(8,128)(2,1)}, bf16[128,4224]{1,0:T(8,128)(2,1)}, u32[]{:S(2)}, u32[]{:S(2)}) collective-permute-start(bf16[128,4224]{1,0:T(8,128)(2,1)} %collective-permute-done.1.refs_0_.refs_3_), channel_id=1, source_target_pairs={{0,1},{1,0},{2,3},{3,2},{4,5},{5,4},{6,7},{7,6},{8,9},{9,8},{10,11... | collective-permute-start | bytes 3244040 | tf_op jit(solution)/shard_map/ppermute | solution.py:308
  85.6 20.1 %collective-permute-start.17 = (bf16[128,4224]{1,0:T(8,128)(2,1)}, bf16[128,4224]{1,0:T(8,128)(2,1)}, u32[]{:S(2)}, u32[]{:S(2)}) collective-permute-start(bf16[128,4224]{1,0:T(8,128)(2,1)} %collective-permute-done.9.refs_1_.refs_4_), channel_id=1, source_target_pairs={{0,1},{1,0},{2,3},{3,2},{4,5},{5,4},{6,7},{7,6},{8,9},{9,8},{10,11... | collective-permute-start | bytes 3244040 | tf_op jit(solution)/shard_map/ppermute | solution.py:308
  90.7 12.5 %collective-permute-start.26 = (bf16[48,4096]{1,0:T(8,128)(2,1)S(1)}, bf16[48,4096]{1,0:T(8,128)(2,1)S(1)}, u32[]{:S(2)}, u32[]{:S(2)}) collective-permute-start(bf16[48,4096]{1,0:T(8,128)(2,1)S(1)} %get-tuple-element.48), channel_id=1, source_target_pairs={{0,16},{16,32},{32,48},{48,0},{1,17},{17,33},{33,49},{49,1},{2,18}... | collective-permute-start | bytes 1179656 | tf_op jit(solution)/shard_map/ppermute | solution.py:308
  91.6 15.2 %collective-permute-start.3 = (bf16[128,4224]{1,0:T(8,128)(2,1)}, bf16[128,4224]{1,0:T(8,128)(2,1)}, u32[]{:S(2)}, u32[]{:S(2)}) collective-permute-start(bf16[128,4224]{1,0:T(8,128)(2,1)} %collective-permute-done.2.refs_0_.refs_5_), channel_id=1, source_target_pairs={{0,2},{1,15},{2,4},{3,1},{4,6},{5,3},{6,8},{7,5},{8,10},{9,7},{10,... | collective-permute-start | bytes 3244040 | tf_op jit(solution)/shard_map/ppermute | solution.py:320
  104.0 21.3 %collective-permute-start.11 = (bf16[128,4224]{1,0:T(8,128)(2,1)}, bf16[128,4224]{1,0:T(8,128)(2,1)}, u32[]{:S(2)}, u32[]{:S(2)}) collective-permute-start(bf16[128,4224]{1,0:T(8,128)(2,1)} %collective-permute-done.2.refs_0_.refs_5_), channel_id=1, source_target_pairs={{0,1},{1,0},{2,3},{3,2},{4,5},{5,4},{6,7},{7,6},{8,9},{9,8},{10,11... | collective-permute-start | bytes 3244040 | tf_op jit(solution)/shard_map/ppermute | solution.py:308
  105.0 22.8 %collective-permute-start.12 = (bf16[128,4224]{1,0:T(8,128)(2,1)}, bf16[128,4224]{1,0:T(8,128)(2,1)}, u32[]{:S(2)}, u32[]{:S(2)}) collective-permute-start(bf16[128,4224]{1,0:T(8,128)(2,1)} %collective-permute-done.10.refs_1_.refs_6_), channel_id=1, source_target_pairs={{0,1},{1,0},{2,3},{3,2},{4,5},{5,4},{6,7},{7,6},{8,9},{9,8},{10,11... | collective-permute-start | bytes 3244040 | tf_op jit(solution)/shard_map/ppermute | solution.py:308
  105.1 12.6 %collective-permute-start.27 = (bf16[48,4096]{1,0:T(8,128)(2,1)}, bf16[48,4096]{1,0:T(8,128)(2,1)S(1)}, u32[]{:S(2)}, u32[]{:S(2)}) collective-permute-start(bf16[48,4096]{1,0:T(8,128)(2,1)} %copy-done.28), channel_id=1, source_target_pairs={{0,32},{16,48},{32,0},{48,16},{1,33},{17,49},{33,1},{49,17},{2,34}... | collective-permute-start | bytes 1179656 | tf_op jit(solution)/shard_map/ppermute | solution.py:308
  105.7 18.9 %collective-permute-start.28 = (bf16[48,4096]{1,0:T(8,128)(2,1)}, bf16[48,4096]{1,0:T(8,128)(2,1)S(1)}, u32[]{:S(2)}, u32[]{:S(2)}) collective-permute-start(bf16[48,4096]{1,0:T(8,128)(2,1)} %copy-done.27), channel_id=1, source_target_pairs={{0,48},{16,0},{32,16},{48,32},{1,49},{17,1},{33,17},{49,33},{2,50}... | collective-permute-start | bytes 1179656 | tf_op jit(solution)/shard_map/ppermute | solution.py:308
  106.7 67.4 %collective-permute-start.4 = (bf16[128,4224]{1,0:T(8,128)(2,1)}, bf16[128,4224]{1,0:T(8,128)(2,1)S(1)}, u32[]{:S(2)}, u32[]{:S(2)}) collective-permute-start(bf16[128,4224]{1,0:T(8,128)(2,1)} %collective-permute-done.3.refs_0_.refs_7_), channel_id=1, source_target_pairs={{0,1},{1,0},{2,3},{3,2},{4,5},{5,4},{6,7},{7,6},{8,9},{9,8},{10,11... | collective-permute-start | bytes 3244040 | tf_op jit(solution)/shard_map/ppermute | solution.py:308
  117.7 15.5 %collective-permute-start.30 = (bf16[48,4096]{1,0:T(8,128)(2,1)S(1)}, bf16[48,4096]{1,0:T(8,128)(2,1)S(1)}, u32[]{:S(2)}, u32[]{:S(2)}) collective-permute-start(bf16[48,4096]{1,0:T(8,128)(2,1)S(1)} %get-tuple-element.52), channel_id=1, source_target_pairs={{0,16},{16,32},{32,48},{48,0},{1,17},{17,33},{33,49},{49,1},{2,18}... | collective-permute-start | bytes 1179656 | tf_op jit(solution)/shard_map/ppermute | solution.py:308
  124.6 15.9 %collective-permute-start.31 = (bf16[48,4096]{1,0:T(8,128)(2,1)S(1)}, bf16[48,4096]{1,0:T(8,128)(2,1)S(1)}, u32[]{:S(2)}, u32[]{:S(2)}) collective-permute-start(bf16[48,4096]{1,0:T(8,128)(2,1)S(1)} %get-tuple-element.53), channel_id=1, source_target_pairs={{0,32},{16,48},{32,0},{48,16},{1,33},{17,49},{33,1},{49,17},{2,34}... | collective-permute-start | bytes 1179656 | tf_op jit(solution)/shard_map/ppermute | solution.py:308
  125.4 20.1 %collective-permute-start.32 = (bf16[48,4096]{1,0:T(8,128)(2,1)S(1)}, bf16[48,4096]{1,0:T(8,128)(2,1)S(1)}, u32[]{:S(2)}, u32[]{:S(2)}) collective-permute-start(bf16[48,4096]{1,0:T(8,128)(2,1)S(1)} %get-tuple-element.54), channel_id=1, source_target_pairs={{0,48},{16,0},{32,16},{48,32},{1,49},{17,1},{33,17},{49,33},{2,50}... | collective-permute-start | bytes 1179656 | tf_op jit(solution)/shard_map/ppermute | solution.py:308
  127.8 28.5 %collective-permute-start.18 = (bf16[96,4096]{1,0:T(8,128)(2,1)S(1)}, bf16[96,4096]{1,0:T(8,128)(2,1)S(1)}, u32[]{:S(2)}, u32[]{:S(2)}) collective-permute-start(bf16[96,4096]{1,0:T(8,128)(2,1)S(1)} %get-tuple-element.40), channel_id=1, source_target_pairs={{0,16},{16,32},{32,48},{48,0},{1,17},{17,33},{33,49},{49,1},{2,18}... | collective-permute-start | bytes 2359304 | tf_op jit(solution)/shard_map/ppermute | solution.py:308
  128.1 46.0 %copy-start.16 = (bf16[48,4096]{1,0:T(8,128)(2,1)S(1)}, bf16[48,4096]{1,0:T(8,128)(2,1)}, u32[]{:S(2)}) copy-start(bf16[48,4096]{1,0:T(8,128)(2,1)} %get-tuple-element.43.refs_0_) | copy-start | bytes 1179652
  128.1 46.0 %copy-start.18 = (bf16[48,4096]{1,0:T(8,128)(2,1)S(1)}, bf16[48,4096]{1,0:T(8,128)(2,1)}, u32[]{:S(2)}) copy-start(bf16[48,4096]{1,0:T(8,128)(2,1)} %copy-done.17) | copy-start | bytes 1179652
  128.1 46.0 %copy-start.20 = (bf16[48,4096]{1,0:T(8,128)(2,1)S(1)}, bf16[48,4096]{1,0:T(8,128)(2,1)}, u32[]{:S(2)}) copy-start(bf16[48,4096]{1,0:T(8,128)(2,1)} %copy-done.19) | copy-start | bytes 1179652
  128.1 46.0 %copy-start.22 = (bf16[48,4096]{1,0:T(8,128)(2,1)S(1)}, bf16[48,4096]{1,0:T(8,128)(2,1)}, u32[]{:S(2)}) copy-start(bf16[48,4096]{1,0:T(8,128)(2,1)} %copy-done.21) | copy-start | bytes 1179652
  128.2 46.0 %copy-start.23 = (bf16[48,4096]{1,0:T(8,128)(2,1)S(1)}, bf16[48,4096]{1,0:T(8,128)(2,1)}, u32[]{:S(2)}) copy-start(bf16[48,4096]{1,0:T(8,128)(2,1)} %get-tuple-element.47.refs_4_) | copy-start | bytes 1179652
  128.2 46.0 %copy-start.25 = (bf16[48,4096]{1,0:T(8,128)(2,1)S(1)}, bf16[48,4096]{1,0:T(8,128)(2,1)}, u32[]{:S(2)}) copy-start(bf16[48,4096]{1,0:T(8,128)(2,1)} %copy-done.24) | copy-start | bytes 1179652
  128.2 46.0 %copy-start.26 = (bf16[48,4096]{1,0:T(8,128)(2,1)S(1)}, bf16[48,4096]{1,0:T(8,128)(2,1)}, u32[]{:S(2)}) copy-start(bf16[48,4096]{1,0:T(8,128)(2,1)} %get-tuple-element.51.refs_8_) | copy-start | bytes 1179652
  133.2 58.2 %collective-permute-start.19 = (bf16[96,4096]{1,0:T(8,128)(2,1)S(1)}, bf16[96,4096]{1,0:T(8,128)(2,1)S(1)}, u32[]{:S(2)}, u32[]{:S(2)}) collective-permute-start(bf16[96,4096]{1,0:T(8,128)(2,1)S(1)} %get-tuple-element.41), channel_id=1, source_target_pairs={{0,32},{16,48},{32,0},{48,16},{1,33},{17,49},{33,1},{49,17},{2,34}... | collective-permute-start | bytes 2359304 | tf_op jit(solution)/shard_map/ppermute | solution.py:308
  140.4 52.3 %collective-permute-start.20 = (bf16[96,4096]{1,0:T(8,128)(2,1)S(1)}, bf16[96,4096]{1,0:T(8,128)(2,1)S(1)}, u32[]{:S(2)}, u32[]{:S(2)}) collective-permute-start(bf16[96,4096]{1,0:T(8,128)(2,1)S(1)} %get-tuple-element.42), channel_id=1, source_target_pairs={{0,48},{16,0},{32,16},{48,32},{1,49},{17,1},{33,17},{49,33},{2,50}... | collective-permute-start | bytes 2359304 | tf_op jit(solution)/shard_map/ppermute | solution.py:308
  145.5 47.3 %collective-permute-start.13 = (bf16[96,4096]{1,0:T(8,128)(2,1)S(1)}, bf16[96,4096]{1,0:T(8,128)(2,1)S(1)}, u32[]{:S(2)}, u32[]{:S(2)}) collective-permute-start(bf16[96,4096]{1,0:T(8,128)(2,1)S(1)} %get-tuple-element.36), channel_id=1, source_target_pairs={{0,16},{16,32},{32,48},{48,0},{1,17},{17,33},{33,49},{49,1},{2,18}... | collective-permute-start | bytes 2359304 | tf_op jit(solution)/shard_map/ppermute | solution.py:308
  156.3 49.7 %collective-permute-start.14 = (bf16[96,4096]{1,0:T(8,128)(2,1)S(1)}, bf16[96,4096]{1,0:T(8,128)(2,1)S(1)}, u32[]{:S(2)}, u32[]{:S(2)}) collective-permute-start(bf16[96,4096]{1,0:T(8,128)(2,1)S(1)} %get-tuple-element.37), channel_id=1, source_target_pairs={{0,32},{16,48},{32,0},{48,16},{1,33},{17,49},{33,1},{49,17},{2,34}... | collective-permute-start | bytes 2359304 | tf_op jit(solution)/shard_map/ppermute | solution.py:308
  174.1 38.7 %collective-permute-start.15 = (bf16[96,4096]{1,0:T(8,128)(2,1)S(1)}, bf16[96,4096]{1,0:T(8,128)(2,1)S(1)}, u32[]{:S(2)}, u32[]{:S(2)}) collective-permute-start(bf16[96,4096]{1,0:T(8,128)(2,1)S(1)} %get-tuple-element.38), channel_id=1, source_target_pairs={{0,48},{16,0},{32,16},{48,32},{1,49},{17,1},{33,17},{49,33},{2,50}... | collective-permute-start | bytes 2359304 | tf_op jit(solution)/shard_map/ppermute | solution.py:308
  191.3 31.7 %collective-permute-start.5 = (bf16[48,4096]{1,0:T(8,128)(2,1)S(1)}, bf16[48,4096]{1,0:T(8,128)(2,1)S(1)}, u32[]{:S(2)}, u32[]{:S(2)}) collective-permute-start(bf16[48,4096]{1,0:T(8,128)(2,1)S(1)} %get-tuple-element.32), channel_id=1, source_target_pairs={{0,16},{16,32},{32,48},{48,0},{1,17},{17,33},{33,49},{49,1},{2,18}... | collective-permute-start | bytes 1179656 | tf_op jit(solution)/shard_map/ppermute | solution.py:308
  192.8 30.2 %collective-permute-start.6 = (bf16[48,4096]{1,0:T(8,128)(2,1)S(1)}, bf16[48,4096]{1,0:T(8,128)(2,1)S(1)}, u32[]{:S(2)}, u32[]{:S(2)}) collective-permute-start(bf16[48,4096]{1,0:T(8,128)(2,1)S(1)} %get-tuple-element.33), channel_id=1, source_target_pairs={{0,32},{16,48},{32,0},{48,16},{1,33},{17,49},{33,1},{49,17},{2,34}... | collective-permute-start | bytes 1179656 | tf_op jit(solution)/shard_map/ppermute | solution.py:308
  192.8 36.6 %collective-permute-start.7 = (bf16[48,4096]{1,0:T(8,128)(2,1)S(1)}, bf16[48,4096]{1,0:T(8,128)(2,1)S(1)}, u32[]{:S(2)}, u32[]{:S(2)}) collective-permute-start(bf16[48,4096]{1,0:T(8,128)(2,1)S(1)} %get-tuple-element.34), channel_id=1, source_target_pairs={{0,48},{16,0},{32,16},{48,32},{1,49},{17,1},{33,17},{49,33},{2,50}... | collective-permute-start | bytes 1179656 | tf_op jit(solution)/shard_map/ppermute | solution.py:308
  234.8 15.6 %all-to-all-start = ((f32[64,2,128]{2,1,0:T(2,128)}), f32[64,2,128]{2,1,0:T(2,128)S(1)}, u32[]{:S(2)}, u32[]{:S(2)}) async-start(f32[64,2,128]{2,1,0:T(2,128)} %bitcast.15), calls=%async_computation | async-start | bytes 131072 | tf_op jit(solution)/shard_map/all_to_all | solution.py:367
  257.2 16.4 %all-to-all-start.1 = ((f32[32,16,128]{2,1,0:T(8,128)}), f32[32,16,128]{2,1,0:T(8,128)S(1)}, u32[]{:S(2)}, u32[]{:S(2)}) async-start(f32[32,16,128]{2,1,0:T(8,128)} %bitcast.17), calls=%async_computation.1 | async-start | bytes 524288 | tf_op jit(solution)/shard_map/all_to_all | solution.py:375
  (25 other events, 195.8 us)
